TPU v7x, 8 devices: a whole 2x2x1 slice. The times are simulated.
8 devices in a mesh: dp: 1 (over z), tp: 8 (over y, x, core).
Axes of the slice: x: 2, y: 2, z: 1, core: 2. Of those that a mesh axis runs over, the one named last changes fastest.
Arguments:
- hidden: bfloat16 [4096, 4096], P(('dp', 'tp'))
- ln_gain: float32 [4096], replicated
- ln_bias: float32 [4096], replicated
- out_embed: bfloat16 [32768, 4096], P('tp')
- vocab_valid: int32 [32768], P('tp')
- targets: int32 [4096], P(('dp', 'tp'))
- loss_mask: int32 [4096], P(('dp', 'tp'))
Outputs:
- output 1: float32 [4096], P(('dp', 'tp'))
- output 2: float32 [1], P('dp')
- output 3: bfloat16 [4096, 4096], P(('dp', 'tp'))
- output 4: float32 [32768, 4096], P(('dp', 'tp'))
- output 5: float32 [4096], P('dp')
- output 6: float32 [4096], P('dp')
All inputs are finite; a program needn't handle non-finite values.
Results may differ from a plain program's by a relative error of at most 0.001.
Values are sent between devices in bfloat16 or wider.
A program may use at most 1 GiB of HBM per device.

v0:
```python
import jax
import jax.numpy as jnp
from jax import lax
from jax.sharding import PartitionSpec as P

SOFT_CAP = 30.0
Z_COEF = 1e-4
LN_EPS = 1e-5


def layer_norm(h_float, ln_gain, ln_bias):
    mean_val = jnp.mean(h_float, axis=-1, keepdims=True)
    centered = h_float - mean_val
    var_val = jnp.mean(centered * centered, axis=-1, keepdims=True)
    return centered * lax.rsqrt(var_val + LN_EPS) * ln_gain + ln_bias


def solution(mesh):
    def group_step(hidden, ln_gain, ln_bias, out_embed, vocab_valid, targets, loss_mask):
        rows_loc = hidden.shape[0]
        vocab_loc = out_embed.shape[0]
        shard_idx = lax.axis_index("tp")
        normed, ln_back = jax.vjp(layer_norm, hidden.astype(jnp.float32), ln_gain, ln_bias)
        x_all = lax.all_gather(normed.astype(jnp.bfloat16), "tp", axis=0, tiled=True)
        tgt_all = lax.all_gather(targets, "tp", axis=0, tiled=True)
        mask_all = lax.all_gather(loss_mask, "tp", axis=0, tiled=True).astype(jnp.float32)
        logits = lax.dot_general(x_all, out_embed, (((1,), (1,)), ((), ())), preferred_element_type=jnp.float32)
        tanh_val = jnp.tanh(logits / SOFT_CAP)
        capped = SOFT_CAP * tanh_val
        col_ok = (vocab_valid != 0)[None, :]
        masked = jnp.where(col_ok, capped, -SOFT_CAP)
        glob_max = lax.pmax(jnp.max(masked, axis=1), "tp")
        exp_vals = jnp.where(col_ok, jnp.exp(masked - glob_max[:, None]), 0.0)
        col_ids = shard_idx * vocab_loc + jnp.arange(vocab_loc)
        is_target = tgt_all[:, None] == col_ids[None, :]
        local_stats = jnp.stack([jnp.sum(exp_vals, axis=1), jnp.sum(jnp.where(is_target, capped, 0.0), axis=1)])
        group_stats = lax.psum(local_stats, "tp")
        sum_exp = group_stats[0]
        lse = glob_max + jnp.log(sum_exp)
        tok_count = jnp.sum(mask_all)
        loss_all = (lse - group_stats[1] + Z_COEF * lse * lse) * mask_all
        mean_loss = jnp.sum(loss_all) / tok_count
        tok_coef = mask_all / tok_count
        prob_coef = (1.0 + 2.0 * Z_COEF * lse) * tok_coef / sum_exp
        d_capped = prob_coef[:, None] * exp_vals - jnp.where(is_target, tok_coef[:, None], 0.0)
        d_logits = (d_capped * (1.0 - tanh_val * tanh_val)).astype(jnp.bfloat16)
        d_embed = lax.dot_general(d_logits, x_all, (((0,), (0,)), ((), ())), preferred_element_type=jnp.float32)
        dx_part = jnp.dot(d_logits, out_embed, preferred_element_type=jnp.float32)
        d_normed = lax.psum_scatter(dx_part, "tp", scatter_dimension=0, tiled=True)
        d_hidden, gain_part, bias_part = ln_back(d_normed)
        d_gain = lax.psum(gain_part, "tp")
        d_bias = lax.psum(bias_part, "tp")
        tok_loss = lax.dynamic_slice_in_dim(loss_all, shard_idx * rows_loc, rows_loc)
        return tok_loss, mean_loss.reshape(1), d_hidden.astype(jnp.bfloat16), d_embed, d_gain, d_bias

    row_spec = P(("dp", "tp"))
    mat_spec = P(("dp", "tp"), None)
    return jax.shard_map(group_step, mesh=mesh, in_specs=(mat_spec, P(None), P(None), P("tp", None), P("tp"), row_spec, row_spec), out_specs=(row_spec, P("dp"), mat_spec, mat_spec, P("dp"), P("dp")), check_vma=False)
```

profile of v0, /device:TPU:0, one launch (start us, length us, event | category | flops | bytes accessed | tf_op | source)
XLA Modules:
  0.0 1043.8 jit_solution(7070638262592237800)
XLA Ops:
  7.2 0.0 all-gather.4.cloned.1.call-start
  7.2 2.8 convert_reduce_fusion
  10.0 0.0 copy-start.4
  10.0 3.4 fusion.15
  13.5 0.0 copy-start.8
  13.5 0.6 copy-done.8
  14.0 0.0 copy-done.4
  14.0 0.0 copy-start.6
  14.0 0.6 copy-done.6
  14.6 5.0 fusion.13
  19.6 0.0 all-gather.4.cloned.1.call-update
  19.7 0.0 reduce-scatter.2.cloned.1.call-start
  19.7 13.6 %all-gather.1 = s32[8,1,512]{2,1,0:T(1,128)S(1)} all-gather(s32[1,1,512]{2,1,0:T(1,128)} %bitcast.22), channel_id=1, replica_groups=mesh['dp'=1,'tp'=8] {'tp'}, dimensions={0}, use_global_device_ids=true | all-gather | bytes 18432 | tf_op jit(solution)/shard_map/all_gather | solution.py:26
  33.4 0.6 convert_element_type.20
  34.0 12.2 %all-gather = s32[8,1,512]{2,1,0:T(1,128)} all-gather(s32[1,1,512]{2,1,0:T(1,128)} %bitcast.23), channel_id=1, replica_groups=mesh['dp'=1,'tp'=8] {'tp'}, dimensions={0}, use_global_device_ids=true | all-gather | bytes 18432 | tf_op jit(solution)/shard_map/all_gather | solution.py:25
  46.2 0.6 iota_add_fusion
  46.8 0.6 convert_reduce_fusion.1
  47.4 0.7 broadcast_compare_fusion
  48.1 129.7 %all-gather.4.cloned.1.call-done = bf16[4096,4096]{1,0:T(8,128)(2,1)} async-done(((bf16[512,4096]{1,0:T(8,128)(2,1)}), bf16[4096,4096]{1,0:T(8,128)(2,1)}) %all-gather.4.cloned.1.call-update) | async-done | bytes 33554448 | tf_op jit(solution)/shard_map/all_gather | solution.py:24
  177.8 0.0 copy-start.1
  177.8 0.0 copy-start.2
  177.8 156.1 %select_reduce_fusion = (f32[4096]{0:T(1024)S(1)}, f32[4096,4096]{0,1:T(8,128)}) fusion(pred[4096]{0:T(1024)(128)(4,1)S(1)} %broadcast_compare_fusion, bf16[4096,4096]{1,0:T(8,128)(2,1)} %all-gather.4.cloned.1.call-done, bf16[4096,4096]{1,0:T(8,128)(2,1)} %param.10), kind=kOutput, calls=%fused_computation.8 | convolution fusion | flops 137506062336 | bytes 134238208 | tf_op jit(solution)/shard_map/dot_general | solution.py:27
  333.9 32.2 %pmax.7 = f32[4096]{0:T(1024)S(1)} all-reduce(f32[4096]{0:T(1024)S(1)} %get-tuple-element.23), channel_id=1, replica_groups=mesh['dp'=1,'tp'=8] {'tp'}, use_global_device_ids=true, to_apply=%region_3.4 | all-reduce | flops 4096 | bytes 32768 | tf_op jit(solution)/shard_map/pmax | solution.py:32
  366.1 0.0 copy-done.1
  366.1 0.0 copy-done.2
  366.1 0.0 copy-start.3
  366.1 34.5 %fusion.5 = (f32[4096]{0:T(1024)S(1)}, f32[4096]{0:T(1024)S(1)}) fusion(f32[4096,4096]{0,1:T(8,128)} %get-tuple-element.24, f32[4096]{0:T(1024)S(1)} %pmax.7, pred[4096]{0:T(1024)(128)(4,1)S(1)} %broadcast_compare_fusion, s32[4096]{0:T(1024)S(1)} %copy-done.2, s32[4096]{0:T(1024)S(1)} %bitcast.15), kind=kLoop, calls=%fused_computation.10 | loop fusion | flops 150986752 | bytes 67194880 | tf_op jit(solution)/shard_map/reduce_sum | solution.py:36
  400.7 24.1 %psum.21 = f32[2,4096]{1,0:T(2,128)S(1)} all-reduce(f32[2,4096]{1,0:T(2,128)S(1)} %pad_maximum_fusion), channel_id=1, replica_groups=mesh['dp'=1,'tp'=8] {'tp'}, use_global_device_ids=true, to_apply=%region_6.7 | all-reduce | flops 8192 | bytes 65536 | tf_op jit(solution)/shard_map/psum | solution.py:37
  424.9 0.0 copy-done.3
  424.9 1.9 multiply_divide_fusion
  426.8 42.6 %fusion.3 = bf16[4096,4096]{0,1:T(8,128)(2,1)} fusion(f32[4096,4096]{0,1:T(8,128)} %get-tuple-element.24, f32[4096]{0:T(1024)S(1)} %get-tuple-element.16, f32[4096]{0:T(1024)S(1)} %get-tuple-element.15, s32[4096]{0:T(1024)S(1)} %bitcast.16, f32[4096]{0:T(1024)S(1)} %pmax.7, s32[4096]{0:T(1024)S(1)} %copy-done.2, pred[4096]{0:T(1024)(128)(4,1)S(1)} %broadcast_compare_fusion), kind=kLoop, calls=%fused_computation.5 | loop fusion | flops 218103808 | bytes 100749312 | tf_op jit(solution)/shard_map/convert_element_type | solution.py:46
  469.4 150.9 %fusion.24 = f32[4096,4096]{1,0:T(8,128)} fusion(bf16[4096,4096]{0,1:T(8,128)(2,1)} %fusion.3, bf16[4096,4096]{1,0:T(8,128)(2,1)} %param.10), kind=kOutput, calls=%fused_computation.44 | convolution fusion | flops 137438953472 | bytes 134217728 | tf_op jit(solution)/shard_map/dot_general | solution.py:48
  620.3 0.0 reduce-scatter.2.cloned.1.call-update
  621.7 1.3 dynamic_slice.3
  623.0 0.0 copy-start
  623.0 0.0 copy-start.5
  623.0 0.0 copy-start.7
  623.1 0.0 copy-start.9
  623.1 154.5 %fusion.25 = f32[4096,4096]{1,0:T(8,128)} fusion(bf16[4096,4096]{0,1:T(8,128)(2,1)} %fusion.3, bf16[4096,4096]{1,0:T(8,128)(2,1)} %all-gather.4.cloned.1.call-done), kind=kOutput, calls=%fused_computation.45 | convolution fusion | flops 137438953472 | bytes 134217728 | tf_op jit(solution)/shard_map/dot_general | solution.py:47
  777.6 219.4 %reduce-scatter.2.cloned.1.call-done = f32[512,4096]{1,0:T(8,128)} async-done(((f32[4096,4096]{1,0:T(8,128)}), f32[512,4096]{1,0:T(8,128)}) %reduce-scatter.2.cloned.1.call-update) | async-done | bytes 8388624 | tf_op jit(solution)/shard_map/reduce_scatter | solution.py:49
  997.0 0.0 copy-done
  997.0 0.0 copy-done.5
  997.0 0.0 copy-done.7
  997.0 6.3 fusion.14
  1003.2 0.0 copy-done.9
  1003.2 5.9 fusion.20
  1009.2 3.3 add_convert_fusion
  1012.5 23.0 %all-reduce = (f32[4096]{0:T(1024)}, f32[4096]{0:T(1024)}) all-reduce(f32[4096]{0:T(1024)S(1)} %get-tuple-element.8, f32[4096]{0:T(1024)S(1)} %get-tuple-element.10), channel_id=1, replica_groups=mesh['dp'=1,'tp'=8] {'tp'}, use_global_device_ids=true, to_apply=%region_13.14 | all-reduce | flops 8192 | bytes 65536 | tf_op jit(solution)/shard_map/psum | solution.py:51
  (6 shorter events, 0.1 us)
Async XLA Ops:
  7.2 170.7 %all-gather.4.cloned.1.call-start = ((), (), s32[]{:S(2)}) async-start(), calls=%async_computation.1 | async-start | bytes 37748736 | tf_op jit(solution)/shard_map/all_gather | solution.py:24
  10.0 4.0 copy-start.4
  13.5 0.6 copy-start.8
  14.0 0.6 copy-start.6
  19.7 977.3 %reduce-scatter.2.cloned.1.call-start = ((), (), s32[]{:S(2)}) async-start(), calls=%async_computation.2 | async-start | bytes 75497472 | tf_op jit(solution)/shard_map/reduce_scatter | solution.py:49
  177.8 188.3 %copy-start.1 = (s32[8,1,512]{2,1,0:T(1,128)S(1)}, s32[8,1,512]{2,1,0:T(1,128)}, u32[]{:S(2)}) copy-start(s32[8,1,512]{2,1,0:T(1,128)} %all-gather) | copy-start | bytes 49156
  177.8 188.3 %copy-start.2 = (s32[4096]{0:T(1024)S(1)}, s32[4096]{0:T(1024)}, u32[]{:S(2)}) copy-start(s32[4096]{0:T(1024)} %iota_add_fusion) | copy-start | bytes 49156
  366.1 58.8 %copy-start.3 = (f32[8,1,512]{2,1,0:T(1,128)S(1)}, f32[8,1,512]{2,1,0:T(1,128)}, u32[]{:S(2)}) copy-start(f32[8,1,512]{2,1,0:T(1,128)} %convert_element_type.20) | copy-start | bytes 49156
  623.0 373.9 %copy-start = (f32[4096]{0:T(1024)S(1)}, f32[4096]{0:T(1024)}, u32[]{:S(2)}) copy-start(f32[4096]{0:T(1024)} %param.8) | copy-start | bytes 49156
  623.0 373.9 %copy-start.5 = (f32[512]{0:T(512)S(1)}, f32[512]{0:T(512)}, u32[]{:S(2)}) copy-start(f32[512]{0:T(512)} %copy-done.4) | copy-start | bytes 6148
  623.0 373.9 %copy-start.7 = (f32[512]{0:T(512)S(1)}, f32[512]{0:T(512)}, u32[]{:S(2)}) copy-start(f32[512]{0:T(512)} %copy-done.6) | copy-start | bytes 6148
  623.1 380.2 %copy-start.9 = (f32[512]{0:T(512)S(1)}, f32[512]{0:T(512)}, u32[]{:S(2)}) copy-start(f32[512]{0:T(512)} %copy-done.8) | copy-start | bytes 6148
Sparse Core Ops, SparseCore 0:
  19.8 157.9 all-gather.3
  620.5 376.4 reduce-scatter.1
where the time goes:
time: 1050 us; the launch traced here: 1040 us
  matrix products  462 us (44%)
  waiting for transfers between devices  349 us (33%)
  other arithmetic  108 us (10%)
  blocking collectives  105 us (10%)
  between operations  17 us (2%)
    reduce_scatter x1, waiting for transfers between devices, group_step(): d_normed = lax.psum_scatter(dx_part, 'tp', scatter_dimension=0, tiled=True)  219 us
    dot_general x1, matrix products, group_step(): lax.dot_general(x_all, out_embed, (((1,), (1,)), ((), ())), preferred_ele...  156 us
    dot_general x1, matrix products, group_step(): lax.dot_general(d_logits, x_all, (((0,), (0,)), ((), ())), preferred_elem...  155 us
    dot_general x1, matrix products, group_step(): dx_part = jnp.dot(d_logits, out_embed, preferred_element_type=jnp.float32)  151 us
    all_gather x1, waiting for transfers between devices, group_step(): lax.all_gather(normed.astype(jnp.bfloat16), 'tp', axis=0, tiled=True)  130 us
    convert_element_type x1, other arithmetic, group_step(): d_logits = (d_capped * (1.0 - tanh_val * tanh_val)).astype(jnp.bfloat16)  42.6 us
    reduce_sum x1, other arithmetic, group_step(): jnp.sum(exp_vals, axis=1)  34.5 us
    pmax x1, blocking collectives, group_step(): glob_max = lax.pmax(jnp.max(masked, axis=1), 'tp')  32.2 us
  transfers between devices with their start and end apart: 2, of which 2 were waited for; matrix products, arithmetic and copies ran while one was open for 15% of the time, Pallas kernels for 0%

commit v1 on v0

v1 whole, which is shorter than its diff:
```python
import jax
import jax.numpy as jnp
from jax import lax
from jax.experimental import pallas as pl
from jax.experimental.pallas import tpu as pltpu
from jax.sharding import PartitionSpec as P


MESH = pl.DeviceIdType.MESH
SOFT_CAP = 30.0
Z_COEF = 1e-4
LN_EPS = 1e-5
PIECE = 128
TV = 1024


def batch_rows(b):
    k1 = b - 4
    k2 = b - 12
    row_a = jnp.where(b < 4, 256 * b, jnp.where(b < 12, (2 + k1 % 2) * 512 + (k1 // 2) * PIECE, (6 + k2 % 2) * 512 + (k2 // 2) * PIECE))
    row_b = jnp.where(b < 4, 256 * b + PIECE, jnp.where(b < 12, (4 + k1 % 2) * 512 + (k1 // 2) * PIECE, (6 + k2 % 2) * 512 + (2 + k2 // 2) * PIECE))
    return row_a, row_b


def static_rows(b):
    if b < 4:
        return 256 * b, 256 * b + PIECE
    if b < 12:
        k = b - 4
        return (2 + k % 2) * 512 + (k // 2) * PIECE, (4 + k % 2) * 512 + (k // 2) * PIECE
    k = b - 12
    return (6 + k % 2) * 512 + (k // 2) * PIECE, (6 + k % 2) * 512 + (2 + k // 2) * PIECE


def logits_kernel(x_own, embed, meta_own, valid, xall, grad, stats, meta, e_vmem, xbuf, acc0, acc1, out, part_s, part_t, mine, others, e_sem, x_sem, g_sem, own_sem, send_sem, recv_sem, meta_send, meta_recv, stat_send, stat_recv):
    me = lax.axis_index("tp")
    tiles = e_vmem.shape[0] // TV
    n_batch = xall.shape[0] // 256

    def peer(bit):
        return {"tp": me ^ bit}

    def fwd(src, row, bit, idx):
        return pltpu.make_async_remote_copy(src_ref=src, dst_ref=xall.at[pl.ds(row, PIECE)], send_sem=send_sem.at[idx], recv_sem=recv_sem.at[idx], device_id=peer(bit), device_id_type=MESH)

    copies = {}
    for p in range(4):
        own = x_own.at[pl.ds(p * PIECE, PIECE)]
        for r in (1, 2, 4):
            copies[r, p] = fwd(own, r * 512 + p * PIECE, r, r * 4 + p)
        copies[3, p] = fwd(xall.at[pl.ds(2 * 512 + p * PIECE, PIECE)], 3 * 512 + p * PIECE, 1, 12 + p)
        copies[5, p] = fwd(xall.at[pl.ds(4 * 512 + p * PIECE, PIECE)], 5 * 512 + p * PIECE, 1, 20 + p)
        via = (2, 4) if p < 2 else (4, 2)
        copies[6, p] = fwd(xall.at[pl.ds(via[0] * 512 + p * PIECE, PIECE)], 6 * 512 + p * PIECE, via[1], 24 + p)
        copies[7, p] = fwd(xall.at[pl.ds(6 * 512 + p * PIECE, PIECE)], 7 * 512 + p * PIECE, 1, 28 + p)

    e_copies = [pltpu.make_async_copy(embed.at[pl.ds(t * TV, TV)], e_vmem.at[pl.ds(t * TV, TV)], e_sem.at[t]) for t in range(tiles)]
    own_loads = [pltpu.make_async_copy(x_own.at[pl.ds(k * 256, 256)], xbuf.at[k], x_sem.at[2 * k]) for k in range(2)]
    own_stores = [pltpu.make_async_copy(xbuf.at[k], xall.at[pl.ds(k * 256, 256)], own_sem.at[k]) for k in range(2)]
    own_loads[0].start()
    e_copies[0].start()
    own_loads[1].start()
    for t in range(1, tiles):
        e_copies[t].start()

    barrier = pltpu.get_barrier_semaphore()
    for bit in range(1, 8):
        pl.semaphore_signal(barrier, inc=1, device_id=peer(bit), device_id_type=MESH)
    pl.semaphore_wait(barrier, 7)
    for p in range(4):
        for r in (2, 4):
            copies[r, p].start()
    for p in range(4):
        copies[1, p].start()
    meta_copies = [pltpu.make_async_remote_copy(src_ref=meta_own, dst_ref=meta.at[bit], send_sem=meta_send.at[bit], recv_sem=meta_recv.at[bit], device_id=peer(bit), device_id_type=MESH) for bit in range(1, 8)]
    for c in meta_copies:
        c.start()
    meta[0] = meta_own[...]
    own_loads[0].wait()
    own_stores[0].start()
    own_loads[1].wait()
    own_stores[1].start()

    def arrive(batch):
        if batch in (2, 3):
            for p in range(2):
                copies[1, 2 * (batch - 2) + p].wait_recv()
        elif 4 <= batch < 12 and batch % 2 == 0:
            p = (batch - 4) // 2
            copies[2, p].wait_recv()
            copies[3, p].start()
            if p < 2:
                copies[6, p].start()
            copies[4, p].wait_recv()
            copies[5, p].start()
            if p >= 2:
                copies[6, p].start()
        elif 4 <= batch < 12:
            p = (batch - 4) // 2
            copies[3, p].wait_recv()
            copies[5, p].wait_recv()
        elif batch % 2 == 0:
            h = (batch - 12) // 2
            for p in (h, 2 + h):
                copies[6, p].wait_recv()
                copies[7, p].start()
        else:
            h = (batch - 12) // 2
            for p in (h, 2 + h):
                copies[7, p].wait_recv()
        if batch == 2:
            for c in meta_copies:
                c.wait_recv()

    def loads(b):
        rows = batch_rows(b)
        slot = b % 2
        return [pltpu.make_async_copy(xall.at[pl.ds(pl.multiple_of(rows[k], PIECE), PIECE)], xbuf.at[slot, pl.ds(k * PIECE, PIECE)], x_sem.at[2 * slot + k]) for k in range(2)]

    row_iota = lax.broadcasted_iota(jnp.int32, (TV, 256), 0)

    def store(b, j):
        rows = batch_rows(b)
        slot = (b + 2) % 2 * tiles + j
        return [pltpu.make_async_copy(out.at[slot, k], grad.at[pl.ds(j * TV, TV), pl.ds(pl.multiple_of(rows[k], PIECE), PIECE)], g_sem.at[2 * slot + k]) for k in range(2)]

    def epilogue(b, j, acc):
        rows = batch_rows(b)
        tgt = jnp.concatenate([meta[rows[k] // 512, pl.ds((rows[k] // PIECE) % 4, 1), :] for k in range(2)], axis=1)
        ok = valid[j * TV:(j + 1) * TV, :]
        t = jnp.tanh(acc[...] * (1.0 / SOFT_CAP))
        e = jnp.exp(t * SOFT_CAP) * ok
        hit = jnp.where(row_iota == tgt - (me * (tiles * TV) + j * TV), t, 0.0)
        g = e * (1.0 - t * t)
        slot = (b + 2) % 2 * tiles + j
        for k in range(2):
            out[slot, k] = g[:, k * PIECE:(k + 1) * PIECE]
        part_s[b * tiles + j] = jnp.sum(e.reshape(TV // 8, 8, 256), axis=0)
        part_t[b * tiles + j] = jnp.sum(hit.reshape(TV // 8, 8, 256), axis=0)

    def dot(b, j, acc):
        acc[...] = lax.dot_general(e_vmem[j * TV:(j + 1) * TV, :], xbuf[b % 2], (((1,), (1,)), ((), ())), preferred_element_type=jnp.float32)

    def body(b, carry):
        before = jnp.maximum(b - 1, 0)

        @pl.when(b == 0)
        def _():
            e_copies[0].wait()
            e_copies[1].wait()

        @pl.when(b >= 2)
        def _():
            for c in loads(b):
                c.wait()

        @pl.when(b >= 3)
        def _():
            for c in store(b - 3, 3):
                c.wait()

        @pl.when(b >= 2)
        def _():
            for j in range(tiles - 1):
                for c in store(b - 2, j):
                    c.wait()

        dot(b, 0, acc0)
        epilogue(before, 3, acc1)
        dot(b, 1, acc1)
        epilogue(b, 0, acc0)

        @pl.when(b == 0)
        def _():
            e_copies[2].wait()
            e_copies[3].wait()
            own_stores[1].wait()

        @pl.when(b == 1)
        def _():
            own_stores[0].wait()

        for nb in range(2, n_batch):
            @pl.when(b == nb - 1)
            def _():
                arrive(nb)

        @pl.when((b >= 1) & (b < n_batch - 1))
        def _():
            for c in loads(b + 1):
                c.start()

        @pl.when(b >= 1)
        def _():
            for c in store(b - 1, 3):
                c.start()

        for c in store(b, 0):
            c.start()
        dot(b, 2, acc0)
        epilogue(b, 1, acc1)
        dot(b, 3, acc1)
        epilogue(b, 2, acc0)
        for j in (1, 2):
            for c in store(b, j):
                c.start()
        return carry

    lax.fori_loop(0, n_batch, body, 0)
    last = n_batch - 1
    for c in store(last - 2, 3):
        c.wait()
    epilogue(last, 3, acc1)
    for c in store(last, 3):
        c.start()
    for b in range(n_batch):
        s_sum = jnp.sum(part_s[b * tiles:(b + 1) * tiles], axis=(0, 1))
        t_sum = jnp.sum(part_t[b * tiles:(b + 1) * tiles], axis=(0, 1))
        for k, row in enumerate(static_rows(b)):
            r, p = row // 512, (row // PIECE) % 4
            mine[r, p:p + 1, :] = s_sum[None, k * PIECE:(k + 1) * PIECE]
            mine[r, 4 + p:5 + p, :] = t_sum[None, k * PIECE:(k + 1) * PIECE]
    for j in range(tiles - 1):
        for c in store(last - 1, j) + store(last, j):
            c.wait()
    for c in store(last - 1, 3) + store(last, 3):
        c.wait()
    stat_copies = [pltpu.make_async_remote_copy(src_ref=mine, dst_ref=others.at[bit - 1], send_sem=stat_send.at[bit], recv_sem=stat_recv.at[bit], device_id=peer(bit), device_id_type=MESH) for bit in range(1, 8)]
    for c in stat_copies:
        c.start()
    for c in meta_copies:
        c.wait_send()
    for c in copies.values():
        c.wait_send()
    for c in stat_copies:
        c.wait()
    for r in range(8):
        t = [mine[r]] + [others[bit - 1, r ^ bit] for bit in range(1, 8)]
        stats[r] = ((t[0] + t[1]) + (t[2] + t[3])) + ((t[4] + t[5]) + (t[6] + t[7]))


def gather_logits(x_own, embed, meta_own, valid):
    rows, dim = x_own.shape
    vocab = embed.shape[0]
    toks = 8 * rows
    any_spec = pl.BlockSpec(memory_space=pl.ANY)
    vmem_spec = pl.BlockSpec(memory_space=pltpu.VMEM)
    steps = toks // 256 * (vocab // TV)
    return pl.pallas_call(
        logits_kernel,
        name="gather_logits",
        out_shape=(jax.ShapeDtypeStruct((toks, dim), jnp.bfloat16), jax.ShapeDtypeStruct((vocab, toks), jnp.float32), jax.ShapeDtypeStruct((8, 8, 128), jnp.float32), jax.ShapeDtypeStruct((8, 8, 128), jnp.int32)),
        in_specs=[any_spec, any_spec, vmem_spec, vmem_spec],
        out_specs=(any_spec, any_spec, vmem_spec, vmem_spec),
        scratch_shapes=[
            pltpu.VMEM((vocab, dim), jnp.bfloat16),
            pltpu.VMEM((2, 256, dim), jnp.bfloat16),
            pltpu.VMEM((TV, 256), jnp.float32),
            pltpu.VMEM((TV, 256), jnp.float32),
            pltpu.VMEM((2 * vocab // TV, 2, TV, PIECE), jnp.float32),
            pltpu.VMEM((steps, 8, 256), jnp.float32),
            pltpu.VMEM((steps, 8, 256), jnp.float32),
            pltpu.VMEM((8, 8, 128), jnp.float32),
            pltpu.VMEM((7, 8, 8, 128), jnp.float32),
            pltpu.SemaphoreType.DMA((vocab // TV,)),
            pltpu.SemaphoreType.DMA((4,)),
            pltpu.SemaphoreType.DMA((4 * vocab // TV,)),
            pltpu.SemaphoreType.DMA((2,)),
            pltpu.SemaphoreType.DMA((32,)),
            pltpu.SemaphoreType.DMA((32,)),
            pltpu.SemaphoreType.DMA((8,)),
            pltpu.SemaphoreType.DMA((8,)),
            pltpu.SemaphoreType.DMA((8,)),
            pltpu.SemaphoreType.DMA((8,)),
        ],
        compiler_params=pltpu.CompilerParams(collective_id=0, has_side_effects=True, vmem_limit_bytes=60 * 1024 * 1024),
        cost_estimate=pl.CostEstimate(flops=2 * toks * vocab * dim, bytes_accessed=vocab * dim * 2 + toks * vocab * 4, transcendentals=2 * toks * vocab),
    )(x_own, embed, meta_own, valid)


def layer_norm(h_float, ln_gain, ln_bias):
    mean_val = jnp.mean(h_float, axis=-1, keepdims=True)
    centered = h_float - mean_val
    var_val = jnp.mean(centered * centered, axis=-1, keepdims=True)
    return centered * lax.rsqrt(var_val + LN_EPS) * ln_gain + ln_bias


def solution(mesh):
    def swap(bit, x):
        return lax.ppermute(x, "tp", [(i, i ^ bit) for i in range(8)])

    def group_step(hidden, ln_gain, ln_bias, out_embed, vocab_valid, targets, loss_mask):
        rows_loc, dim = hidden.shape
        vocab_loc = out_embed.shape[0]
        shard_idx = lax.axis_index("tp")
        normed, ln_back = jax.vjp(layer_norm, hidden.astype(jnp.float32), ln_gain, ln_bias)
        meta_own = jnp.concatenate([targets.reshape(4, PIECE), loss_mask.reshape(4, PIECE)])
        x_all, grad, stats, meta = gather_logits(normed.astype(jnp.bfloat16), out_embed, meta_own, (vocab_valid != 0).astype(jnp.float32)[:, None])
        sum_exp = stats[:, :4].reshape(8, rows_loc)
        tgt_tanh = stats[:, 4:].reshape(8, rows_loc)
        tgt_row = meta[:, :4].reshape(8 * rows_loc) - shard_idx * vocab_loc
        mask_all = meta[:, 4:].reshape(8, rows_loc).astype(jnp.float32)

        def group_sum(part):
            return ((part[0] + part[1]) + (part[2] + part[3])) + ((part[4] + part[5]) + (part[6] + part[7]))

        tok_count = group_sum(jnp.sum(mask_all, axis=1))
        lse = jnp.log(sum_exp)
        loss_all = (lse - SOFT_CAP * tgt_tanh + Z_COEF * lse * lse) * mask_all
        mean_loss = group_sum(jnp.sum(loss_all, axis=1)) / tok_count
        tok_coef = mask_all / tok_count
        prob_coef = ((1.0 + 2.0 * Z_COEF * lse) * tok_coef / sum_exp).reshape(1, 8 * rows_loc)
        tgt_coef = (tok_coef * (1.0 - tgt_tanh * tgt_tanh)).reshape(1, 8 * rows_loc)
        is_target = tgt_row[None, :] == jnp.arange(vocab_loc)[:, None]
        d_logits = (prob_coef * grad - jnp.where(is_target, tgt_coef, 0.0)).astype(jnp.bfloat16)
        d_logits = lax.optimization_barrier(d_logits)

        mid = dim // 2

        def part(d_log, r, c):
            rows = d_log[:, r * rows_loc:(r + 1) * rows_loc]
            return lax.dot_general(rows, out_embed[:, c * mid:(c + 1) * mid], (((0,), (0,)), ((), ())), preferred_element_type=jnp.float32)

        def after(d_log, *done):
            return lax.optimization_barrier((d_log, *done))

        far = [part(d_logits, 7, c) for c in range(2)]
        step, *far = after(d_logits, *far)
        pair_far = [part(step, 6, c) + swap(1, far[c]) for c in range(2)]
        step, *pair_far = after(step, *pair_far)
        to_x, to_y = swap(2, pair_far[0]), swap(4, pair_far[1])
        near = [part(step, 3, 0), part(step, 5, 1), part(step, 3, 1), part(step, 5, 0)]
        step, *near = after(step, *near)
        late = [swap(1, near[2]), swap(1, near[3])]
        early = [swap(1, near[0]), swap(1, near[1])]
        first = [part(step, 2, 0) + early[0], part(step, 4, 1) + early[1]]
        step, *first = after(step, *first)
        from_x, from_y = [swap(2, first[0]), None], [None, swap(4, first[1])]
        other = [part(step, 1, c) for c in range(2)]
        step, *other = after(step, *other)
        own = [part(step, 0, c) + swap(1, other[c]) for c in range(2)]
        step, *own = after(step, *own)
        second = [part(step, 2, 1) + late[0] + to_y, part(step, 4, 0) + late[1] + to_x]
        step, *second = after(step, *second)
        from_x[1], from_y[0] = swap(2, second[0]), swap(4, second[1])
        d_embed = lax.dot_general(step, x_all, (((1,), (0,)), ((), ())), preferred_element_type=jnp.float32)
        d_normed = jnp.concatenate([own[c] + from_x[c] + from_y[c] for c in range(2)], axis=1)
        d_hidden, gain_part, bias_part = ln_back(d_normed)
        d_both = lax.psum(jnp.stack([gain_part, bias_part]), "tp")
        tok_loss = loss_all[0]
        return tok_loss, mean_loss.reshape(1), d_hidden.astype(jnp.bfloat16), d_embed, d_both[0], d_both[1]

    row_spec = P(("dp", "tp"))
    mat_spec = P(("dp", "tp"), None)

    return jax.shard_map(group_step, mesh=mesh, in_specs=(mat_spec, P(None), P(None), P("tp", None), P("tp"), row_spec, row_spec), out_specs=(row_spec, P("dp"), mat_spec, mat_spec, P("dp"), P("dp")), check_vma=False)
```

time: 1050 us -> 834 us (0.79)
  waiting for transfers between devices: 349 us -> 63.9 us
  Pallas kernels: 0 us -> 256 us
  blocking collectives: 105 us -> 22.4 us
  matrix products: 462 us -> 380 us
  other arithmetic: 108 us -> 84.9 us
    pallas_call x0 -> x1, Pallas kernels: none -> 256 us  [gather_logits(): pl.pallas_call(logits_kernel, name='gather_logits', out_shape=(jax.ShapeD...]
    reduce_scatter x1 -> x0, waiting for transfers between devices: 219 us -> none  [group_step(): d_normed = lax.psum_scatter(dx_part, 'tp', scatter_dimension=0, tiled=True)]
    all_gather x1 -> x0, waiting for transfers between devices: 130 us -> none  [group_step(): lax.all_gather(normed.astype(jnp.bfloat16), 'tp', axis=0, tiled=True)]
    dot_general x3 -> x17, matrix products: 462 us -> 380 us  [the longest x16 229 us: part(): lax.dot_general(rows, out_embed[:, c * mid:(c + 1) * mid], (((0,), (0,)),...]
    ppermute x0 -> x14, waiting for transfers between devices: none -> 63.9 us  [swap(): return lax.ppermute(x, 'tp', [(i, i ^ bit) for i in range(8)])]
    reduce_sum x2 -> x0, other arithmetic: 35.2 us -> none  [the longest x1 34.5 us: group_step(): jnp.sum(exp_vals, axis=1)]
    pmax x1 -> x0, blocking collectives: 32.2 us -> none  [group_step(): glob_max = lax.pmax(jnp.max(masked, axis=1), 'tp')]
    all_gather x2 -> x0, blocking collectives: 25.8 us -> none  [the longest x1 13.6 us: group_step(): lax.all_gather(loss_mask, 'tp', axis=0, tiled=True).astype(jnp.float32)]
  transfers between devices with their start and end apart: 2 -> 14, of which waited for: 2 -> 5; matrix products, arithmetic and copies ran while one was open for 15% -> 31% of each run, Pallas kernels for 0% -> 0%
where the time goes in v1:
time: 834 us; the launch traced here: 831 us
  matrix products  380 us (46%)
  Pallas kernels  256 us (31%)
  other arithmetic  84.9 us (10%)
  waiting for transfers between devices  63.9 us (8%)
  blocking collectives  22.4 us (3%)
  between operations  12.5 us (1%)
    pallas_call x1, Pallas kernels, gather_logits(): pl.pallas_call(logits_kernel, name='gather_logits', out_shape=(jax.ShapeD...  256 us
    dot_general x16, matrix products, part(): lax.dot_general(rows, out_embed[:, c * mid:(c + 1) * mid], (((0,), (0,)),...  229 us
    dot_general x1, matrix products, group_step(): lax.dot_general(step, x_all, (((1,), (0,)), ((), ())), preferred_element_...  151 us
    ppermute x14, waiting for transfers between devices, swap(): return lax.ppermute(x, 'tp', [(i, i ^ bit) for i in range(8)])  63.9 us
    convert_element_type x1, other arithmetic, group_step(): (prob_coef * grad - jnp.where(is_target, tgt_coef, 0.0)).astype(jnp.bfloa...  33.6 us
    psum x1, blocking collectives, group_step(): d_both = lax.psum(jnp.stack([gain_part, bias_part]), 'tp')  22.4 us
  transfers between devices with their start and end apart: 14, of which 5 were waited for; matrix products, arithmetic and copies ran while one was open for 31% of the time, Pallas kernels for 0%

profile of v1, /device:TPU:0, one launch (start us, length us, event | category | flops | bytes accessed | tf_op | source)
XLA Modules:
  0.0 830.9 jit_solution(1183129121920586110)
XLA Ops:
  0.7 2.8 convert_reduce_fusion
  3.5 3.4 fusion.9
  7.0 0.6 copy-done.13
  7.6 2.0 copy.13.valid
  9.5 0.6 pad_add_fusion.meta_own
  10.1 5.5 fusion.7.x_own
  15.7 255.7 %gather_logits.1 = (bf16[4096,4096]{1,0:T(8,128)(2,1)}, f32[4096,4096]{1,0:T(8,128)}, f32[8,8,128]{2,1,0:T(8,128)}, s32[8,8,128]{2,1,0:T(8,128)}) custom-call(bf16[512,4096]{1,0:T(8,128)(2,1)} %fusion.7.x_own, bf16[4096,4096]{1,0:T(8,128)(2,1)} %embed.1, s32[8,128]{1,0:T(8,128)} %pad_add_fusion.meta_own, f32[4096,1]{1,0:T(8,128)} %copy.13.valid), custom_call_target="tpu_custom_call" | custom-call | flops 137438953472 | bytes 100663296 | tf_op jit(solution)/shard_map/gather_logits/pallas_call | solution.py:249
  271.4 1.5 slice_subtract_fusion
  272.9 1.5 fusion.86
  274.3 0.7 fusion.87
  280.1 0.8 convert_divide_fusion
  280.9 33.6 %subtract_convert_fusion = bf16[4096,4096]{1,0:T(8,128)(2,1)} fusion(f32[4096,4096]{1,0:T(8,128)} %get-tuple-element.35, f32[4096]{0:T(1024)S(1)} %get-tuple-element.78, s32[4096]{0:T(1024)S(1)} %bitcast.31, f32[4096]{0:T(1024)S(1)} %get-tuple-element.77), kind=kLoop, calls=%fused_computation | loop fusion | flops 83886080 | bytes 100712448 | tf_op jit(solution)/shard_map/convert_element_type | solution.py:315
  314.5 13.1 %fusion.20 = f32[512,2048]{1,0:T(8,128)S(1)} fusion(bf16[4096,4096]{1,0:T(8,128)(2,1)} %subtract_convert_fusion, bf16[4096,4096]{1,0:T(8,128)(2,1)} %embed.1), kind=kOutput, calls=%fused_computation.31 | convolution fusion | flops 8589934592 | bytes 25165824 | tf_op jit(solution)/shard_map/dot_general | solution.py:322
  327.6 12.9 %fusion.22 = f32[512,2048]{1,0:T(8,128)S(1)} fusion(bf16[4096,4096]{1,0:T(8,128)(2,1)} %subtract_convert_fusion, bf16[4096,4096]{1,0:T(8,128)(2,1)} %embed.1), kind=kOutput, calls=%fused_computation.33 | convolution fusion | flops 8589934592 | bytes 25165824 | tf_op jit(solution)/shard_map/dot_general | solution.py:322
  341.1 6.6 collective-permute-done
  347.7 15.0 %fusion.44 = f32[512,2048]{1,0:T(8,128)} fusion(f32[512,2048]{1,0:T(8,128)S(1)} %collective-permute-done, bf16[4096,4096]{1,0:T(8,128)(2,1)} %subtract_convert_fusion, bf16[4096,4096]{1,0:T(8,128)(2,1)} %embed.1), kind=kOutput, calls=%fused_computation.55 | convolution fusion | flops 8590983168 | bytes 29360128 | tf_op jit(solution)/shard_map/dot_general | solution.py:322
  362.7 14.9 %fusion.47 = f32[512,2048]{1,0:T(8,128)} fusion(f32[512,2048]{1,0:T(8,128)S(1)} %collective-permute-done.1, bf16[4096,4096]{1,0:T(8,128)(2,1)} %subtract_convert_fusion, bf16[4096,4096]{1,0:T(8,128)(2,1)} %embed.1), kind=kOutput, calls=%fused_computation.56 | convolution fusion | flops 8590983168 | bytes 29360128 | tf_op jit(solution)/shard_map/dot_general | solution.py:322
  377.7 15.0 %fusion.36 = f32[512,2048]{1,0:T(8,128)} fusion(bf16[4096,4096]{1,0:T(8,128)(2,1)} %subtract_convert_fusion, bf16[4096,4096]{1,0:T(8,128)(2,1)} %embed.1), kind=kOutput, calls=%fused_computation.47 | convolution fusion | flops 8589934592 | bytes 25165824 | tf_op jit(solution)/shard_map/dot_general | solution.py:322
  392.6 15.2 %fusion.32 = f32[512,2048]{1,0:T(8,128)} fusion(bf16[4096,4096]{1,0:T(8,128)(2,1)} %subtract_convert_fusion, bf16[4096,4096]{1,0:T(8,128)(2,1)} %embed.1), kind=kOutput, calls=%fused_computation.43 | convolution fusion | flops 8589934592 | bytes 25165824 | tf_op jit(solution)/shard_map/dot_general | solution.py:322
  407.8 12.9 %fusion.34 = f32[512,2048]{1,0:T(8,128)S(1)} fusion(bf16[4096,4096]{1,0:T(8,128)(2,1)} %subtract_convert_fusion, bf16[4096,4096]{1,0:T(8,128)(2,1)} %embed.1), kind=kOutput, calls=%fused_computation.45 | convolution fusion | flops 8589934592 | bytes 25165824 | tf_op jit(solution)/shard_map/dot_general | solution.py:322
  420.7 12.9 %fusion.38 = f32[512,2048]{1,0:T(8,128)S(1)} fusion(bf16[4096,4096]{1,0:T(8,128)(2,1)} %subtract_convert_fusion, bf16[4096,4096]{1,0:T(8,128)(2,1)} %embed.1), kind=kOutput, calls=%fused_computation.49 | convolution fusion | flops 8589934592 | bytes 25165824 | tf_op jit(solution)/shard_map/dot_general | solution.py:322
  434.2 6.6 collective-permute-done.2
  440.8 15.0 %fusion.56 = f32[512,2048]{1,0:T(8,128)} fusion(f32[512,2048]{1,0:T(8,128)S(1)} %collective-permute-done.2, bf16[4096,4096]{1,0:T(8,128)(2,1)} %subtract_convert_fusion, bf16[4096,4096]{1,0:T(8,128)(2,1)} %embed.1), kind=kOutput, calls=%fused_computation.59 | convolution fusion | flops 8590983168 | bytes 29360128 | tf_op jit(solution)/shard_map/dot_general | solution.py:322
  455.8 14.9 %fusion.59 = f32[512,2048]{1,0:T(8,128)} fusion(f32[512,2048]{1,0:T(8,128)S(1)} %collective-permute-done.3, bf16[4096,4096]{1,0:T(8,128)(2,1)} %subtract_convert_fusion, bf16[4096,4096]{1,0:T(8,128)(2,1)} %embed.1), kind=kOutput, calls=%fused_computation.60 | convolution fusion | flops 8590983168 | bytes 29360128 | tf_op jit(solution)/shard_map/dot_general | solution.py:322
  470.8 15.3 %fusion.28 = f32[512,2048]{1,0:T(8,128)} fusion(bf16[4096,4096]{1,0:T(8,128)(2,1)} %subtract_convert_fusion, bf16[4096,4096]{1,0:T(8,128)(2,1)} %embed.1), kind=kOutput, calls=%fused_computation.39 | convolution fusion | flops 8589934592 | bytes 25165824 | tf_op jit(solution)/shard_map/dot_general | solution.py:322
  486.1 15.0 %fusion.30 = f32[512,2048]{1,0:T(8,128)} fusion(bf16[4096,4096]{1,0:T(8,128)(2,1)} %subtract_convert_fusion, bf16[4096,4096]{1,0:T(8,128)(2,1)} %embed.1), kind=kOutput, calls=%fused_computation.41 | convolution fusion | flops 8589934592 | bytes 25165824 | tf_op jit(solution)/shard_map/dot_general | solution.py:322
  506.7 0.6 fusion.82
  508.6 0.6 collective-permute-start.10
  509.2 15.6 %fusion.50 = f32[512,2048]{1,0:T(8,128)} fusion(f32[512,2048]{1,0:T(8,128)} %collective-permute-done.4, bf16[4096,4096]{1,0:T(8,128)(2,1)} %subtract_convert_fusion, bf16[4096,4096]{1,0:T(8,128)(2,1)} %embed.1), kind=kOutput, calls=%fused_computation.57 | convolution fusion | flops 8590983168 | bytes 29360128 | tf_op jit(solution)/shard_map/dot_general | solution.py:322
  524.7 1.4 collective-permute-start.6
  526.2 15.7 %fusion.53 = f32[512,2048]{1,0:T(8,128)} fusion(f32[512,2048]{1,0:T(8,128)} %collective-permute-done.5, bf16[4096,4096]{1,0:T(8,128)(2,1)} %subtract_convert_fusion, bf16[4096,4096]{1,0:T(8,128)(2,1)} %embed.1), kind=kOutput, calls=%fused_computation.58 | convolution fusion | flops 8590983168 | bytes 29360128 | tf_op jit(solution)/shard_map/dot_general | solution.py:322
  541.9 12.9 %fusion.13 = f32[512,2048]{1,0:T(8,128)S(1)} fusion(bf16[4096,4096]{1,0:T(8,128)(2,1)} %subtract_convert_fusion, bf16[4096,4096]{1,0:T(8,128)(2,1)} %embed.1), kind=kOutput, calls=%fused_computation.23 | convolution fusion | flops 8589934592 | bytes 25165824 | tf_op jit(solution)/shard_map/dot_general | solution.py:322
  554.9 1.2 collective-permute-start.13
  556.1 45.4 %collective-permute-done.8 = f32[512,2048]{1,0:T(8,128)} collective-permute-done((f32[512,2048]{1,0:T(8,128)}, f32[512,2048]{1,0:T(8,128)}, u32[]{:S(2)}, u32[]{:S(2)}) %collective-permute-start.8) | collective-permute-done | bytes 4194336 | tf_op jit(solution)/shard_map/ppermute | solution.py:290
  601.5 5.4 add_add_fusion.3
  607.0 12.9 %fusion.11 = f32[512,2048]{1,0:T(8,128)S(1)} fusion(bf16[4096,4096]{1,0:T(8,128)(2,1)} %subtract_convert_fusion, bf16[4096,4096]{1,0:T(8,128)(2,1)} %embed.1), kind=kOutput, calls=%fused_computation.20 | convolution fusion | flops 8589934592 | bytes 25165824 | tf_op jit(solution)/shard_map/dot_general | solution.py:322
  619.9 3.4 add_add_fusion.2
  623.3 0.6 collective-permute-start.11
  623.8 0.6 collective-permute-start.12
  624.4 151.2 %fusion.89 = f32[4096,4096]{1,0:T(8,128)} fusion(bf16[4096,4096]{1,0:T(8,128)(2,1)} %subtract_convert_fusion, bf16[4096,4096]{1,0:T(8,128)(2,1)} %get-tuple-element.59), kind=kOutput, calls=%fused_computation.109 | convolution fusion | flops 137438953472 | bytes 134217728 | tf_op jit(solution)/shard_map/dot_general | solution.py:346
  775.6 4.9 collective-permute-done.11
  780.5 6.0 add_add_fusion.4
  786.6 6.4 add_add_fusion.1
  793.1 4.1 fusion.8
  797.2 22.4 %psum.7 = f32[2,4096]{1,0:T(2,128)S(1)} all-reduce(f32[2,4096]{1,0:T(2,128)S(1)} %pad_maximum_fusion.1), channel_id=1, replica_groups=mesh['dp'=1,'tp'=8] {'tp'}, use_global_device_ids=true, to_apply=%region_8.9 | all-reduce | flops 8192 | bytes 65536 | tf_op jit(solution)/shard_map/psum | solution.py:349
  819.6 5.9 fusion.84
  825.6 0.6 fusion.85
  826.2 3.3 add_convert_fusion
  (65 shorter events, 3.1 us)
Async XLA Ops:
  0.6 6.9 copy-start.16
  0.6 8.9 %copy-start.17 = (s32[512]{0:T(512)S(1)}, s32[512]{0:T(512)}, u32[]{:S(2)}) copy-start(s32[512]{0:T(512)} %param.13) | copy-start | bytes 6148
  0.7 8.9 %copy-start.18 = (s32[512]{0:T(512)S(1)}, s32[512]{0:T(512)}, u32[]{:S(2)}) copy-start(s32[512]{0:T(512)} %param.12) | copy-start | bytes 6148
  0.7 9.5 %copy-start.4 = (f32[4096]{0:T(1024)S(1)}, f32[4096]{0:T(1024)}, u32[]{:S(2)}) copy-start(f32[4096]{0:T(1024)} %param.8) | copy-start | bytes 49156
  0.7 9.5 %copy-start.15 = (f32[4096]{0:T(1024)S(1)}, f32[4096]{0:T(1024)}, u32[]{:S(2)}) copy-start(f32[4096]{0:T(1024)} %param.9) | copy-start | bytes 49156
  3.5 267.9 %copy-start.9 = (f32[512]{0:T(512)}, f32[512]{0:T(512)S(1)}, u32[]{:S(2)}) copy-start(f32[512]{0:T(512)S(1)} %broadcast_multiply_fusion) | copy-start | bytes 6148
  7.0 0.6 copy-start.13
  7.5 263.8 %copy-start.11 = (f32[512]{0:T(512)}, f32[512]{0:T(512)S(1)}, u32[]{:S(2)}) copy-start(f32[512]{0:T(512)S(1)} %fusion.83) | copy-start | bytes 6148
  340.6 7.2 collective-permute-start
  340.8 22.0 %collective-permute-start.1 = (f32[512,2048]{1,0:T(8,128)S(1)}, f32[512,2048]{1,0:T(8,128)S(1)}, u32[]{:S(2)}, u32[]{:S(2)}) collective-permute-start(f32[512,2048]{1,0:T(8,128)S(1)} %fusion.20), channel_id=1, source_target_pairs={{0,1},{1,0},{2,3},{3,2},{4,5},{5,4},{6,7},{7,6}} | collective-permute-start | bytes 12582920 | tf_op jit(solution)/shard_map/ppermute | solution.py:290
  433.7 7.2 collective-permute-start.2
  433.9 21.9 %collective-permute-start.3 = (f32[512,2048]{1,0:T(8,128)S(1)}, f32[512,2048]{1,0:T(8,128)S(1)}, u32[]{:S(2)}, u32[]{:S(2)}) collective-permute-start(f32[512,2048]{1,0:T(8,128)S(1)} %fusion.34), channel_id=1, source_target_pairs={{0,1},{1,0},{2,3},{3,2},{4,5},{5,4},{6,7},{7,6}} | collective-permute-start | bytes 12582920 | tf_op jit(solution)/shard_map/ppermute | solution.py:290
  486.1 15.5 %copy-start.8 = (f32[1,8,4,128]{3,2,1,0:T(4,128)S(1)}, f32[1,8,4,128]{3,2,1,0:T(4,128)}, u32[]{:S(2)}) copy-start(f32[1,8,4,128]{3,2,1,0:T(4,128)} %get-tuple-element.76) | copy-start | bytes 49156
  486.1 20.6 %copy-start.6 = (f32[1,8,4,128]{3,2,1,0:T(4,128)S(1)}, f32[1,8,4,128]{3,2,1,0:T(4,128)}, u32[]{:S(2)}) copy-start(f32[1,8,4,128]{3,2,1,0:T(4,128)} %get-tuple-element.70) | copy-start | bytes 49156
  486.1 20.6 %copy-start.7 = (f32[1,8,4,128]{3,2,1,0:T(4,128)S(1)}, f32[1,8,4,128]{3,2,1,0:T(4,128)}, u32[]{:S(2)}) copy-start(f32[1,8,4,128]{3,2,1,0:T(4,128)} %get-tuple-element.74) | copy-start | bytes 49156
  501.1 7.5 collective-permute-start.4
  501.3 23.5 %collective-permute-start.5 = (f32[512,2048]{1,0:T(8,128)}, f32[512,2048]{1,0:T(8,128)}, u32[]{:S(2)}, u32[]{:S(2)}) collective-permute-start(f32[512,2048]{1,0:T(8,128)} %fusion.28), channel_id=1, source_target_pairs={{0,1},{1,0},{2,3},{3,2},{4,5},{5,4},{6,7},{7,6}} | collective-permute-start | bytes 12582920 | tf_op jit(solution)/shard_map/ppermute | solution.py:290
  507.3 47.6 %collective-permute-start.7 = (f32[512,2048]{1,0:T(8,128)}, f32[512,2048]{1,0:T(8,128)S(1)}, u32[]{:S(2)}, u32[]{:S(2)}) collective-permute-start(f32[512,2048]{1,0:T(8,128)} %fusion.36), channel_id=1, source_target_pairs={{0,1},{1,0},{2,3},{3,2},{4,5},{5,4},{6,7},{7,6}} | collective-permute-start | bytes 12582920 | tf_op jit(solution)/shard_map/ppermute | solution.py:290
  507.4 112.4 %collective-permute-start.9 = (f32[512,2048]{1,0:T(8,128)}, f32[512,2048]{1,0:T(8,128)S(1)}, u32[]{:S(2)}, u32[]{:S(2)}) collective-permute-start(f32[512,2048]{1,0:T(8,128)} %fusion.32), channel_id=1, source_target_pairs={{0,1},{1,0},{2,3},{3,2},{4,5},{5,4},{6,7},{7,6}} | collective-permute-start | bytes 12582920 | tf_op jit(solution)/shard_map/ppermute | solution.py:290
  507.8 93.8 %collective-permute-start.8 = (f32[512,2048]{1,0:T(8,128)}, f32[512,2048]{1,0:T(8,128)}, u32[]{:S(2)}, u32[]{:S(2)}) collective-permute-start(f32[512,2048]{1,0:T(8,128)} %fusion.47), channel_id=1, source_target_pairs={{0,4},{1,5},{2,6},{3,7},{4,0},{5,1},{6,2},{7,3}} | collective-permute-start | bytes 12582920 | tf_op jit(solution)/shard_map/ppermute | solution.py:290
  508.6 111.3 %collective-permute-start.10 = (f32[512,2048]{1,0:T(8,128)}, f32[512,2048]{1,0:T(8,128)S(1)}, u32[]{:S(2)}, u32[]{:S(2)}) collective-permute-start(f32[512,2048]{1,0:T(8,128)} %fusion.44), channel_id=1, source_target_pairs={{0,2},{1,3},{2,0},{3,1},{4,6},{5,7},{6,4},{7,5}} | collective-permute-start | bytes 12582920 | tf_op jit(solution)/shard_map/ppermute | solution.py:290
  524.7 250.8 %collective-permute-start.6 = (f32[512,2048]{1,0:T(8,128)}, f32[512,2048]{1,0:T(8,128)}, u32[]{:S(2)}, u32[]{:S(2)}) collective-permute-start(f32[512,2048]{1,0:T(8,128)} %fusion.56), channel_id=1, source_target_pairs={{0,2},{1,3},{2,0},{3,1},{4,6},{5,7},{6,4},{7,5}} | collective-permute-start | bytes 12582920 | tf_op jit(solution)/shard_map/ppermute | solution.py:290
  554.9 231.7 %collective-permute-start.13 = (f32[512,2048]{1,0:T(8,128)}, f32[512,2048]{1,0:T(8,128)}, u32[]{:S(2)}, u32[]{:S(2)}) collective-permute-start(f32[512,2048]{1,0:T(8,128)} %fusion.59), channel_id=1, source_target_pairs={{0,4},{1,5},{2,6},{3,7},{4,0},{5,1},{6,2},{7,3}} | collective-permute-start | bytes 12582920 | tf_op jit(solution)/shard_map/ppermute | solution.py:290
  623.3 157.2 %collective-permute-start.11 = (f32[512,2048]{1,0:T(8,128)}, f32[512,2048]{1,0:T(8,128)}, u32[]{:S(2)}, u32[]{:S(2)}) collective-permute-start(f32[512,2048]{1,0:T(8,128)} %add_add_fusion.2), channel_id=1, source_target_pairs={{0,4},{1,5},{2,6},{3,7},{4,0},{5,1},{6,2},{7,3}} | collective-permute-start | bytes 12582920 | tf_op jit(solution)/shard_map/ppermute | solution.py:290
  623.8 162.7 %collective-permute-start.12 = (f32[512,2048]{1,0:T(8,128)}, f32[512,2048]{1,0:T(8,128)}, u32[]{:S(2)}, u32[]{:S(2)}) collective-permute-start(f32[512,2048]{1,0:T(8,128)} %add_add_fusion.3), channel_id=1, source_target_pairs={{0,2},{1,3},{2,0},{3,1},{4,6},{5,7},{6,4},{7,5}} | collective-permute-start | bytes 12582920 | tf_op jit(solution)/shard_map/ppermute | solution.py:290
  775.6 11.0 %copy-start.3 = (f32[512,2048]{1,0:T(8,128)S(1)}, f32[512,2048]{1,0:T(8,128)}, u32[]{:S(2)}) copy-start(f32[512,2048]{1,0:T(8,128)} %fusion.53) | copy-start | bytes 12582916
  786.5 6.5 copy-start.1
  786.5 6.5 copy-start
  786.5 6.5 copy-start.5
  786.5 6.5 copy-start.10
  786.5 6.5 copy-start.12
  793.1 4.1 copy-start.2
  793.1 26.5 %copy-start.14 = (f32[512]{0:T(512)S(1)}, f32[512]{0:T(512)}, u32[]{:S(2)}) copy-start(f32[512]{0:T(512)} %copy-done.13) | copy-start | bytes 6148

commit v2 on v1

--- a/solution.py
+++ b/solution.py
@@ -1,3 +1,5 @@
+import functools
+
 import jax
 import jax.numpy as jnp
 from jax import lax
@@ -67,9 +69,8 @@
     for bit in range(1, 8):
         pl.semaphore_signal(barrier, inc=1, device_id=peer(bit), device_id_type=MESH)
     pl.semaphore_wait(barrier, 7)
-    for p in range(4):
-        for r in (2, 4):
-            copies[r, p].start()
+    for r in (2, 4):
+        copies[r, 0].start()
     for p in range(4):
         copies[1, p].start()
     meta_copies = [pltpu.make_async_remote_copy(src_ref=meta_own, dst_ref=meta.at[bit], send_sem=meta_send.at[bit], recv_sem=meta_recv.at[bit], device_id=peer(bit), device_id_type=MESH) for bit in range(1, 8)]
@@ -82,19 +83,22 @@
     own_stores[1].start()
 
     def arrive(batch):
+        if batch in (2, 4, 6):
+            for r in (2, 4):
+                copies[r, batch // 2].start()
+        elif batch in (8, 10):
+            copies[6, batch // 2 - 4].start()
         if batch in (2, 3):
             for p in range(2):
                 copies[1, 2 * (batch - 2) + p].wait_recv()
         elif 4 <= batch < 12 and batch % 2 == 0:
             p = (batch - 4) // 2
+            copies[4, p].wait_recv()
+            if p >= 2:
+                copies[6, p].start()
+            copies[5, p].start()
             copies[2, p].wait_recv()
             copies[3, p].start()
-            if p < 2:
-                copies[6, p].start()
-            copies[4, p].wait_recv()
-            copies[5, p].start()
-            if p >= 2:
-                copies[6, p].start()
         elif 4 <= batch < 12:
             p = (batch - 4) // 2
             copies[3, p].wait_recv()
@@ -278,6 +282,35 @@
     )(x_own, embed, meta_own, valid)
 
 
+def part_kernel(n_add, d_log, embed, *refs):
+    adds, outs = refs[:n_add], refs[n_add:]
+    j = pl.program_id(0)
+    half = pl.num_programs(0) // 2
+    val = lax.dot_general(d_log[...], embed[...], (((0,), (0,)), ((), ())), preferred_element_type=jnp.float32)
+    for c in range(2):
+        @pl.when(j // half == c)
+        def _():
+            outs[c][...] = val + adds[c][...] if adds else val
+
+
+def dx_part(d_log, embed, r, adds=()):
+    vocab, dim = embed.shape
+    rows, tile = 512, 512
+    half = dim // tile // 2
+    maps = [lambda j: (0, jnp.minimum(j, half - 1)), lambda j: (0, jnp.maximum(j - half, 0))]
+    specs = [pl.BlockSpec((rows, tile), m) for m in maps]
+    return pl.pallas_call(
+        functools.partial(part_kernel, len(adds)),
+        name="dx_part",
+        grid=(2 * half,),
+        out_shape=[jax.ShapeDtypeStruct((rows, dim // 2), jnp.float32)] * 2,
+        in_specs=[pl.BlockSpec((vocab, rows), lambda j: (0, r)), pl.BlockSpec((vocab, tile), lambda j: (0, j))] + specs[:len(adds)],
+        out_specs=specs,
+        compiler_params=pltpu.CompilerParams(vmem_limit_bytes=48 * 1024 * 1024),
+        cost_estimate=pl.CostEstimate(flops=2 * rows * vocab * dim, bytes_accessed=vocab * (rows + dim) * 2 + rows * dim * 4 * (1 + len(adds) // 2), transcendentals=0),
+    )(d_log, embed, *adds)
+
+
 def layer_norm(h_float, ln_gain, ln_bias):
     mean_val = jnp.mean(h_float, axis=-1, keepdims=True)
     centered = h_float - mean_val
@@ -329,18 +362,20 @@
         pair_far = [part(step, 6, c) + swap(1, far[c]) for c in range(2)]
         step, *pair_far = after(step, *pair_far)
         to_x, to_y = swap(2, pair_far[0]), swap(4, pair_far[1])
-        near = [part(step, 3, 0), part(step, 5, 1), part(step, 3, 1), part(step, 5, 0)]
+        near = [*dx_part(step, out_embed, 3), *dx_part(step, out_embed, 5)]
         step, *near = after(step, *near)
-        late = [swap(1, near[2]), swap(1, near[3])]
-        early = [swap(1, near[0]), swap(1, near[1])]
-        first = [part(step, 2, 0) + early[0], part(step, 4, 1) + early[1]]
-        step, *first = after(step, *first)
-        from_x, from_y = [swap(2, first[0]), None], [None, swap(4, first[1])]
-        other = [part(step, 1, c) for c in range(2)]
+        other = dx_part(step, out_embed, 1)
+        got = [swap(1, x) for x in near]
         step, *other = after(step, *other)
-        own = [part(step, 0, c) + swap(1, other[c]) for c in range(2)]
+        first_x = dx_part(step, out_embed, 2, got[:2])
+        step, *first_x = after(step, *first_x)
+        first_y = dx_part(step, out_embed, 4, got[2:])
+        step, *first_y = after(step, *first_y)
+        from_x, from_y = [swap(2, first_x[0]), None], [None, swap(4, first_y[1])]
+        got = [swap(1, x) for x in other]
+        own = dx_part(step, out_embed, 0, got)
         step, *own = after(step, *own)
-        second = [part(step, 2, 1) + late[0] + to_y, part(step, 4, 0) + late[1] + to_x]
+        second = [first_x[1] + to_y, first_y[0] + to_x]
         step, *second = after(step, *second)
         from_x[1], from_y[0] = swap(2, second[0]), swap(4, second[1])
         d_embed = lax.dot_general(step, x_all, (((1,), (0,)), ((), ())), preferred_element_type=jnp.float32)

time: 834 us -> 721 us (0.86)
  matrix products: 380 us -> 208 us
  Pallas kernels: 256 us -> 342 us
  waiting for transfers between devices: 63.9 us -> 34 us
    dot_general x16 -> x4, matrix products: 229 us -> 56.7 us  [part(): lax.dot_general(rows, out_embed[:, c * mid:(c + 1) * mid], (((0,), (0,)),...]
    pallas_call x0 -> x6, Pallas kernels: none -> 153 us  [dx_part(): pl.pallas_call(functools.partial(part_kernel, len(adds)), name='dx_part',...]
    pallas_call x1, Pallas kernels: 256 us -> 189 us  [gather_logits(): pl.pallas_call(logits_kernel, name='gather_logits', out_shape=(jax.ShapeD...]
    ppermute x14, waiting for transfers between devices: 63.9 us -> 34 us  [swap(): return lax.ppermute(x, 'tp', [(i, i ^ bit) for i in range(8)])]
  transfers between devices with their start and end apart: 14 -> 14, of which waited for: 5 -> 3; matrix products, arithmetic and copies ran while one was open for 31% -> 26% of each run, Pallas kernels for 0% -> 14%
where the time goes in v2:
time: 721 us; the launch traced here: 717 us
  Pallas kernels  342 us (47%)
  matrix products  208 us (29%)
  other arithmetic  85.5 us (12%)
  waiting for transfers between devices  34 us (5%)
  blocking collectives  22.4 us (3%)
  between operations  12.5 us (2%)
    pallas_call x1, Pallas kernels, gather_logits(): pl.pallas_call(logits_kernel, name='gather_logits', out_shape=(jax.ShapeD...  189 us
    pallas_call x6, Pallas kernels, dx_part(): pl.pallas_call(functools.partial(part_kernel, len(adds)), name='dx_part',...  153 us
    dot_general x1, matrix products, group_step(): lax.dot_general(step, x_all, (((1,), (0,)), ((), ())), preferred_element_...  151 us
    dot_general x4, matrix products, part(): lax.dot_general(rows, out_embed[:, c * mid:(c + 1) * mid], (((0,), (0,)),...  56.7 us
    ppermute x14, waiting for transfers between devices, swap(): return lax.ppermute(x, 'tp', [(i, i ^ bit) for i in range(8)])  34 us
    convert_element_type x1, other arithmetic, group_step(): (prob_coef * grad - jnp.where(is_target, tgt_coef, 0.0)).astype(jnp.bfloa...  33.6 us
    psum x1, blocking collectives, group_step(): d_both = lax.psum(jnp.stack([gain_part, bias_part]), 'tp')  22.4 us
  transfers between devices with their start and end apart: 14, of which 3 were waited for; matrix products, arithmetic and copies ran while one was open for 26% of the time, Pallas kernels for 14%

profile of v2, /device:TPU:0, one launch (start us, length us, event | category | flops | bytes accessed | tf_op | source)
XLA Modules:
  0.0 717.2 jit_solution(14891846844717489623)
XLA Ops:
  0.7 2.8 convert_reduce_fusion
  3.5 3.4 fusion.17
  7.0 0.6 copy-done.12
  7.6 2.0 copy.13.valid
  9.5 0.6 pad_add_fusion.meta_own
  10.1 5.5 fusion.15.x_own
  15.7 189.0 %gather_logits.1 = (bf16[4096,4096]{1,0:T(8,128)(2,1)}, f32[4096,4096]{1,0:T(8,128)}, f32[8,8,128]{2,1,0:T(8,128)}, s32[8,8,128]{2,1,0:T(8,128)}) custom-call(bf16[512,4096]{1,0:T(8,128)(2,1)} %fusion.15.x_own, bf16[4096,4096]{1,0:T(8,128)(2,1)} %embed.13, s32[8,128]{1,0:T(8,128)} %pad_add_fusion.meta_own, f32[4096,1]{1,0:T(8,128)} %copy.13.valid), custom_call_target="tpu_custom_call" | custom-call | flops 137438953472 | bytes 100663296 | tf_op jit(solution)/shard_map/gather_logits/pallas_call | solution.py:253
  204.7 0.8 slice_subtract_fusion
  205.6 1.0 fusion.42
  206.5 0.7 fusion.43
  212.4 0.8 convert_divide_fusion
  213.2 33.6 %subtract_convert_fusion.d_log = bf16[4096,4096]{1,0:T(8,128)(2,1)} fusion(f32[4096,4096]{1,0:T(8,128)} %get-tuple-element.50, f32[4096]{0:T(1024)S(1)} %get-tuple-element.108, s32[4096]{0:T(1024)S(1)} %bitcast.31, f32[4096]{0:T(1024)S(1)} %get-tuple-element.107), kind=kLoop, calls=%fused_computation | loop fusion | flops 83886080 | bytes 100712448 | tf_op jit(solution)/shard_map/convert_element_type | solution.py:348
  246.8 13.1 %fusion.2 = f32[512,2048]{1,0:T(8,128)S(1)} fusion(bf16[4096,4096]{1,0:T(8,128)(2,1)} %embed.13, bf16[4096,4096]{1,0:T(8,128)(2,1)} %subtract_convert_fusion.d_log), kind=kOutput, calls=%fused_computation.4 | convolution fusion | flops 8589934592 | bytes 25165824 | tf_op jit(solution)/shard_map/dot_general | solution.py:355
  259.9 12.9 %fusion.6 = f32[512,2048]{1,0:T(8,128)S(1)} fusion(bf16[4096,4096]{1,0:T(8,128)(2,1)} %embed.13, bf16[4096,4096]{1,0:T(8,128)(2,1)} %subtract_convert_fusion.d_log), kind=kOutput, calls=%fused_computation.8 | convolution fusion | flops 8589934592 | bytes 25165824 | tf_op jit(solution)/shard_map/dot_general | solution.py:355
  272.8 0.2 collective-permute-start
  273.0 0.3 collective-permute-start.1
  273.4 6.8 collective-permute-done
  280.1 15.6 %fusion.24 = f32[512,2048]{1,0:T(8,128)} fusion(f32[512,2048]{1,0:T(8,128)} %collective-permute-done, bf16[4096,4096]{1,0:T(8,128)(2,1)} %embed.13, bf16[4096,4096]{1,0:T(8,128)(2,1)} %subtract_convert_fusion.d_log), kind=kOutput, calls=%fused_computation.33 | convolution fusion | flops 8590983168 | bytes 29360128 | tf_op jit(solution)/shard_map/dot_general | solution.py:355
  295.8 15.1 %fusion.29 = f32[512,2048]{1,0:T(8,128)} fusion(f32[512,2048]{1,0:T(8,128)S(1)} %collective-permute-done.1, bf16[4096,4096]{1,0:T(8,128)(2,1)} %embed.13, bf16[4096,4096]{1,0:T(8,128)(2,1)} %subtract_convert_fusion.d_log), kind=kOutput, calls=%fused_computation.34 | convolution fusion | flops 8590983168 | bytes 29360128 | tf_op jit(solution)/shard_map/dot_general | solution.py:355
  310.9 24.7 %dx_part.7 = (f32[512,2048]{1,0:T(8,128)}, f32[512,2048]{1,0:T(8,128)}) custom-call(bf16[4096,4096]{1,0:T(8,128)(2,1)} %subtract_convert_fusion.d_log, bf16[4096,4096]{1,0:T(8,128)(2,1)} %embed.13), custom_call_target="tpu_custom_call" | custom-call | flops 17179869184 | bytes 46137344 | tf_op jit(solution)/shard_map/dx_part/pallas_call | solution.py:302
  335.5 24.7 %dx_part.6 = (f32[512,2048]{1,0:T(8,128)S(1)}, f32[512,2048]{1,0:T(8,128)}) custom-call(bf16[4096,4096]{1,0:T(8,128)(2,1)} %subtract_convert_fusion.d_log, bf16[4096,4096]{1,0:T(8,128)(2,1)} %embed.13), custom_call_target="tpu_custom_call" | custom-call | flops 17179869184 | bytes 46137344 | tf_op jit(solution)/shard_map/dx_part/pallas_call | solution.py:302
  360.4 0.3 collective-permute-start.3
  360.9 0.3 collective-permute-start.5
  361.2 24.7 %dx_part.8 = (f32[512,2048]{1,0:T(8,128)}, f32[512,2048]{1,0:T(8,128)}) custom-call(bf16[4096,4096]{1,0:T(8,128)(2,1)} %subtract_convert_fusion.d_log, bf16[4096,4096]{1,0:T(8,128)(2,1)} %embed.13), custom_call_target="tpu_custom_call" | custom-call | flops 17179869184 | bytes 46137344 | tf_op jit(solution)/shard_map/dx_part/pallas_call | solution.py:302
  386.1 2.1 copy-done.4
  388.2 0.3 collective-permute-start.7
  393.6 0.6 fusion.38
  394.2 0.4 collective-permute-start.9
  394.6 0.4 collective-permute-start.10
  395.0 26.7 %dx_part.9 = (f32[512,2048]{1,0:T(8,128)}, f32[512,2048]{1,0:T(8,128)}) custom-call(bf16[4096,4096]{1,0:T(8,128)(2,1)} %subtract_convert_fusion.d_log, bf16[4096,4096]{1,0:T(8,128)(2,1)} %embed.13, f32[512,2048]{1,0:T(8,128)} %copy-done.4, f32[512,2048]{1,0:T(8,128)} %collective-permute-done.3.refs_1_), custom_call_target="tpu_custom_call" | custom-call | flops 17179869184 | bytes 54525952 | tf_op jit(solution)/shard_map/dx_part/pallas_call | solution.py:302
  421.6 26.0 %dx_part.10 = (f32[512,2048]{1,0:T(8,128)S(1)}, f32[512,2048]{1,0:T(8,128)}) custom-call(bf16[4096,4096]{1,0:T(8,128)(2,1)} %subtract_convert_fusion.d_log, bf16[4096,4096]{1,0:T(8,128)(2,1)} %embed.13, f32[512,2048]{1,0:T(8,128)} %collective-permute-done.4.refs_0_, f32[512,2048]{1,0:T(8,128)} %collective-permute-done.5.refs_1_), custom_call_target="tpu_custom_call" | custom-call | flops 17179869184 | bytes 54525952 | tf_op jit(solution)/shard_map/dx_part/pallas_call | solution.py:302
  447.7 1.9 collective-permute-start.13
  449.5 1.4 collective-permute-start.8
  450.9 26.1 %dx_part.11 = (f32[512,2048]{1,0:T(8,128)S(1)}, f32[512,2048]{1,0:T(8,128)}) custom-call(bf16[4096,4096]{1,0:T(8,128)(2,1)} %subtract_convert_fusion.d_log, bf16[4096,4096]{1,0:T(8,128)(2,1)} %embed.13, f32[512,2048]{1,0:T(8,128)} %collective-permute-done.6.refs_0_, f32[512,2048]{1,0:T(8,128)} %collective-permute-done.7.refs_1_), custom_call_target="tpu_custom_call" | custom-call | flops 17179869184 | bytes 54525952 | tf_op jit(solution)/shard_map/dx_part/pallas_call | solution.py:302
  477.0 10.8 %collective-permute-done.9 = f32[512,2048]{1,0:T(8,128)S(1)} collective-permute-done((f32[512,2048]{1,0:T(8,128)}, f32[512,2048]{1,0:T(8,128)S(1)}, u32[]{:S(2)}, u32[]{:S(2)}) %collective-permute-start.9) | collective-permute-done | bytes 4194336 | tf_op jit(solution)/shard_map/ppermute | solution.py:323
  487.8 5.3 add.146
  493.1 5.3 add.147
  498.4 0.4 collective-permute-start.11
  498.9 0.4 collective-permute-start.12
  499.2 151.4 %fusion.45 = f32[4096,4096]{1,0:T(8,128)} fusion(bf16[4096,4096]{1,0:T(8,128)(2,1)} %subtract_convert_fusion.d_log, bf16[4096,4096]{1,0:T(8,128)(2,1)} %get-tuple-element.89), kind=kOutput, calls=%fused_computation.67 | convolution fusion | flops 137438953472 | bytes 134217728 | tf_op jit(solution)/shard_map/dot_general | solution.py:381
  650.6 16.3 %collective-permute-done.11 = f32[512,2048]{1,0:T(8,128)} collective-permute-done((f32[512,2048]{1,0:T(8,128)}, f32[512,2048]{1,0:T(8,128)}, u32[]{:S(2)}, u32[]{:S(2)}) %collective-permute-start.11) | collective-permute-done | bytes 4194336 | tf_op jit(solution)/shard_map/ppermute | solution.py:323
  666.9 6.0 add_add_fusion.2
  673.0 6.4 add_add_fusion.1
  679.5 4.0 fusion.16
  683.6 22.4 %psum.7 = f32[2,4096]{1,0:T(2,128)S(1)} all-reduce(f32[2,4096]{1,0:T(2,128)S(1)} %pad_maximum_fusion.1), channel_id=1, replica_groups=mesh['dp'=1,'tp'=8] {'tp'}, use_global_device_ids=true, to_apply=%region_8.9 | all-reduce | flops 8192 | bytes 65536 | tf_op jit(solution)/shard_map/psum | solution.py:384
  706.0 5.9 fusion.40
  711.9 0.6 fusion.41
  712.6 3.3 add_convert_fusion
  (57 shorter events, 0.7 us)
Async XLA Ops:
  0.6 6.9 copy-start.15
  0.6 8.9 %copy-start.16 = (s32[512]{0:T(512)S(1)}, s32[512]{0:T(512)}, u32[]{:S(2)}) copy-start(s32[512]{0:T(512)} %param.13) | copy-start | bytes 6148
  0.7 8.9 %copy-start.17 = (s32[512]{0:T(512)S(1)}, s32[512]{0:T(512)}, u32[]{:S(2)}) copy-start(s32[512]{0:T(512)} %param.12) | copy-start | bytes 6148
  0.7 9.5 %copy-start.6 = (f32[4096]{0:T(1024)S(1)}, f32[4096]{0:T(1024)}, u32[]{:S(2)}) copy-start(f32[4096]{0:T(1024)} %param.8) | copy-start | bytes 49156
  0.7 9.5 %copy-start.14 = (f32[4096]{0:T(1024)S(1)}, f32[4096]{0:T(1024)}, u32[]{:S(2)}) copy-start(f32[4096]{0:T(1024)} %param.9) | copy-start | bytes 49156
  3.5 201.2 %copy-start.8 = (f32[512]{0:T(512)}, f32[512]{0:T(512)S(1)}, u32[]{:S(2)}) copy-start(f32[512]{0:T(512)S(1)} %broadcast_multiply_fusion) | copy-start | bytes 6148
  7.0 0.6 copy-start.12
  7.5 197.1 %copy-start.10 = (f32[512]{0:T(512)}, f32[512]{0:T(512)S(1)}, u32[]{:S(2)}) copy-start(f32[512]{0:T(512)S(1)} %fusion.39) | copy-start | bytes 6148
  272.8 7.3 %collective-permute-start = (f32[512,2048]{1,0:T(8,128)S(1)}, f32[512,2048]{1,0:T(8,128)}, u32[]{:S(2)}, u32[]{:S(2)}) collective-permute-start(f32[512,2048]{1,0:T(8,128)S(1)} %fusion.6), channel_id=1, source_target_pairs={{0,1},{1,0},{2,3},{3,2},{4,5},{5,4},{6,7},{7,6}} | collective-permute-start | bytes 12582920 | tf_op jit(solution)/shard_map/ppermute | solution.py:323
  273.0 22.8 %collective-permute-start.1 = (f32[512,2048]{1,0:T(8,128)S(1)}, f32[512,2048]{1,0:T(8,128)S(1)}, u32[]{:S(2)}, u32[]{:S(2)}) collective-permute-start(f32[512,2048]{1,0:T(8,128)S(1)} %fusion.2), channel_id=1, source_target_pairs={{0,1},{1,0},{2,3},{3,2},{4,5},{5,4},{6,7},{7,6}} | collective-permute-start | bytes 12582920 | tf_op jit(solution)/shard_map/ppermute | solution.py:323
  360.2 25.9 %collective-permute-start.2 = (f32[512,2048]{1,0:T(8,128)S(1)}, f32[512,2048]{1,0:T(8,128)S(1)}, u32[]{:S(2)}, u32[]{:S(2)}) collective-permute-start(f32[512,2048]{1,0:T(8,128)S(1)} %get-tuple-element.63), channel_id=1, source_target_pairs={{0,1},{1,0},{2,3},{3,2},{4,5},{5,4},{6,7},{7,6}} | collective-permute-start | bytes 12582920 | tf_op jit(solution)/shard_map/ppermute | solution.py:323
  360.4 33.8 %collective-permute-start.3 = (f32[512,2048]{1,0:T(8,128)}, f32[512,2048]{1,0:T(8,128)}, u32[]{:S(2)}, u32[]{:S(2)}) collective-permute-start(f32[512,2048]{1,0:T(8,128)} %get-tuple-element.64), channel_id=1, source_target_pairs={{0,1},{1,0},{2,3},{3,2},{4,5},{5,4},{6,7},{7,6}} | collective-permute-start | bytes 12582920 | tf_op jit(solution)/shard_map/ppermute | solution.py:323
  360.7 33.9 %collective-permute-start.4 = (f32[512,2048]{1,0:T(8,128)}, f32[512,2048]{1,0:T(8,128)}, u32[]{:S(2)}, u32[]{:S(2)}) collective-permute-start(f32[512,2048]{1,0:T(8,128)} %get-tuple-element.68), channel_id=1, source_target_pairs={{0,1},{1,0},{2,3},{3,2},{4,5},{5,4},{6,7},{7,6}} | collective-permute-start | bytes 12582920 | tf_op jit(solution)/shard_map/ppermute | solution.py:323
  360.9 60.7 %collective-permute-start.5 = (f32[512,2048]{1,0:T(8,128)}, f32[512,2048]{1,0:T(8,128)}, u32[]{:S(2)}, u32[]{:S(2)}) collective-permute-start(f32[512,2048]{1,0:T(8,128)} %get-tuple-element.69), channel_id=1, source_target_pairs={{0,1},{1,0},{2,3},{3,2},{4,5},{5,4},{6,7},{7,6}} | collective-permute-start | bytes 12582920 | tf_op jit(solution)/shard_map/ppermute | solution.py:323
  386.0 63.6 %collective-permute-start.6 = (f32[512,2048]{1,0:T(8,128)}, f32[512,2048]{1,0:T(8,128)}, u32[]{:S(2)}, u32[]{:S(2)}) collective-permute-start(f32[512,2048]{1,0:T(8,128)} %get-tuple-element.73), channel_id=1, source_target_pairs={{0,1},{1,0},{2,3},{3,2},{4,5},{5,4},{6,7},{7,6}} | collective-permute-start | bytes 12582920 | tf_op jit(solution)/shard_map/ppermute | solution.py:323
  386.1 2.1 copy-start.4
  388.2 62.7 %collective-permute-start.7 = (f32[512,2048]{1,0:T(8,128)}, f32[512,2048]{1,0:T(8,128)}, u32[]{:S(2)}, u32[]{:S(2)}) collective-permute-start(f32[512,2048]{1,0:T(8,128)} %get-tuple-element.74), channel_id=1, source_target_pairs={{0,1},{1,0},{2,3},{3,2},{4,5},{5,4},{6,7},{7,6}} | collective-permute-start | bytes 12582920 | tf_op jit(solution)/shard_map/ppermute | solution.py:323
  394.2 93.7 %collective-permute-start.9 = (f32[512,2048]{1,0:T(8,128)}, f32[512,2048]{1,0:T(8,128)S(1)}, u32[]{:S(2)}, u32[]{:S(2)}) collective-permute-start(f32[512,2048]{1,0:T(8,128)} %fusion.29), channel_id=1, source_target_pairs={{0,4},{1,5},{2,6},{3,7},{4,0},{5,1},{6,2},{7,3}} | collective-permute-start | bytes 12582920 | tf_op jit(solution)/shard_map/ppermute | solution.py:323
  394.6 98.5 %collective-permute-start.10 = (f32[512,2048]{1,0:T(8,128)}, f32[512,2048]{1,0:T(8,128)}, u32[]{:S(2)}, u32[]{:S(2)}) collective-permute-start(f32[512,2048]{1,0:T(8,128)} %fusion.24), channel_id=1, source_target_pairs={{0,2},{1,3},{2,0},{3,1},{4,6},{5,7},{6,4},{7,5}} | collective-permute-start | bytes 12582920 | tf_op jit(solution)/shard_map/ppermute | solution.py:323
  447.7 225.3 %collective-permute-start.13 = (f32[512,2048]{1,0:T(8,128)}, f32[512,2048]{1,0:T(8,128)}, u32[]{:S(2)}, u32[]{:S(2)}) collective-permute-start(f32[512,2048]{1,0:T(8,128)} %get-tuple-element.87), channel_id=1, source_target_pairs={{0,4},{1,5},{2,6},{3,7},{4,0},{5,1},{6,2},{7,3}} | collective-permute-start | bytes 12582920 | tf_op jit(solution)/shard_map/ppermute | solution.py:323
  449.5 201.1 %collective-permute-start.8 = (f32[512,2048]{1,0:T(8,128)}, f32[512,2048]{1,0:T(8,128)}, u32[]{:S(2)}, u32[]{:S(2)}) collective-permute-start(f32[512,2048]{1,0:T(8,128)} %get-tuple-element.78), channel_id=1, source_target_pairs={{0,2},{1,3},{2,0},{3,1},{4,6},{5,7},{6,4},{7,5}} | collective-permute-start | bytes 12582920 | tf_op jit(solution)/shard_map/ppermute | solution.py:323
  477.0 21.4 %copy-start = (f32[512,2048]{1,0:T(8,128)}, f32[512,2048]{1,0:T(8,128)S(1)}, u32[]{:S(2)}) copy-start(f32[512,2048]{1,0:T(8,128)S(1)} %get-tuple-element.77) | copy-start | bytes 12582916
  498.4 168.5 %collective-permute-start.11 = (f32[512,2048]{1,0:T(8,128)}, f32[512,2048]{1,0:T(8,128)}, u32[]{:S(2)}, u32[]{:S(2)}) collective-permute-start(f32[512,2048]{1,0:T(8,128)} %add.147), channel_id=1, source_target_pairs={{0,4},{1,5},{2,6},{3,7},{4,0},{5,1},{6,2},{7,3}} | collective-permute-start | bytes 12582920 | tf_op jit(solution)/shard_map/ppermute | solution.py:323
  498.9 174.1 %collective-permute-start.12 = (f32[512,2048]{1,0:T(8,128)}, f32[512,2048]{1,0:T(8,128)}, u32[]{:S(2)}, u32[]{:S(2)}) collective-permute-start(f32[512,2048]{1,0:T(8,128)} %add.146), channel_id=1, source_target_pairs={{0,2},{1,3},{2,0},{3,1},{4,6},{5,7},{6,4},{7,5}} | collective-permute-start | bytes 12582920 | tf_op jit(solution)/shard_map/ppermute | solution.py:323
  650.6 22.4 %copy-start.5 = (f32[512,2048]{1,0:T(8,128)S(1)}, f32[512,2048]{1,0:T(8,128)}, u32[]{:S(2)}) copy-start(f32[512,2048]{1,0:T(8,128)} %get-tuple-element.85) | copy-start | bytes 12582916
  672.9 6.5 copy-start.2
  672.9 6.5 copy-start.1
  672.9 6.5 copy-start.7
  672.9 6.5 copy-start.9
  673.0 6.5 copy-start.11
  679.5 4.0 copy-start.3
  679.5 26.5 %copy-start.13 = (f32[512]{0:T(512)S(1)}, f32[512]{0:T(512)}, u32[]{:S(2)}) copy-start(f32[512]{0:T(512)} %copy-done.12) | copy-start | bytes 6148

commit v3 on v2

--- a/solution.py
+++ b/solution.py
@@ -282,33 +282,111 @@
     )(x_own, embed, meta_own, valid)
 
 
-def part_kernel(n_add, d_log, embed, *refs):
-    adds, outs = refs[:n_add], refs[n_add:]
+def part_kernel(n_dev, n_add, *refs):
+    d_logs, embed = refs[:n_dev], refs[n_dev]
+    adds, outs = refs[n_dev + 1:n_dev + 1 + n_add], refs[n_dev + 1 + n_add:]
     j = pl.program_id(0)
     half = pl.num_programs(0) // 2
-    val = lax.dot_general(d_log[...], embed[...], (((0,), (0,)), ((), ())), preferred_element_type=jnp.float32)
+    vals = [lax.dot_general(d[...], embed[...], (((0,), (0,)), ((), ())), preferred_element_type=jnp.float32) for d in d_logs]
     for c in range(2):
         @pl.when(j // half == c)
         def _():
-            outs[c][...] = val + adds[c][...] if adds else val
-
-
-def dx_part(d_log, embed, r, adds=()):
+            for q, val in enumerate(vals):
+                outs[2 * q + c][...] = val + adds[2 * q + c][...] if adds else val
+
+
+def dx_part(d_log, embed, devs, adds=()):
     vocab, dim = embed.shape
     rows, tile = 512, 512
     half = dim // tile // 2
     maps = [lambda j: (0, jnp.minimum(j, half - 1)), lambda j: (0, jnp.maximum(j - half, 0))]
-    specs = [pl.BlockSpec((rows, tile), m) for m in maps]
+    specs = [pl.BlockSpec((rows, tile), m) for m in maps] * len(devs)
     return pl.pallas_call(
-        functools.partial(part_kernel, len(adds)),
+        functools.partial(part_kernel, len(devs), len(adds)),
         name="dx_part",
         grid=(2 * half,),
-        out_shape=[jax.ShapeDtypeStruct((rows, dim // 2), jnp.float32)] * 2,
-        in_specs=[pl.BlockSpec((vocab, rows), lambda j: (0, r)), pl.BlockSpec((vocab, tile), lambda j: (0, j))] + specs[:len(adds)],
+        out_shape=[jax.ShapeDtypeStruct((rows, dim // 2), jnp.float32)] * (2 * len(devs)),
+        in_specs=[pl.BlockSpec((vocab, rows), lambda j, r=r: (0, r)) for r in devs] + [pl.BlockSpec((vocab, tile), lambda j: (0, j))] + specs[:len(adds)],
         out_specs=specs,
-        compiler_params=pltpu.CompilerParams(vmem_limit_bytes=48 * 1024 * 1024),
-        cost_estimate=pl.CostEstimate(flops=2 * rows * vocab * dim, bytes_accessed=vocab * (rows + dim) * 2 + rows * dim * 4 * (1 + len(adds) // 2), transcendentals=0),
-    )(d_log, embed, *adds)
+        compiler_params=pltpu.CompilerParams(vmem_limit_bytes=60 * 1024 * 1024),
+        cost_estimate=pl.CostEstimate(flops=2 * len(devs) * rows * vocab * dim, bytes_accessed=vocab * (len(devs) * rows + dim) * 2 + len(devs) * rows * dim * 4 * (2 if adds else 1), transcendentals=0),
+    )(*[d_log] * len(devs), embed, *adds)
+
+
+def norm_back_kernel(own_a, own_b, x_a, x_b, y_a, y_b, hidden, gain, d_hidden, sums, acc):
+    step = pl.program_id(0)
+    h = hidden[...].astype(jnp.float32)
+    dim = h.shape[1]
+    centered = h - jnp.sum(h, axis=1, keepdims=True) * (1.0 / dim)
+    rstd = lax.rsqrt(jnp.sum(centered * centered, axis=1, keepdims=True) * (1.0 / dim) + LN_EPS)
+    xh = centered * rstd
+    d_normed = jnp.concatenate([own_a[...] + x_a[...] + y_a[...], own_b[...] + x_b[...] + y_b[...]], axis=1)
+    d_gain = d_normed * xh
+    rows = h.shape[0]
+
+    @pl.when(step == 0)
+    def _():
+        acc[...] = jnp.zeros_like(acc)
+
+    acc[0] += jnp.sum(d_gain.reshape(rows // 8, 8, dim), axis=0)
+    acc[1] += jnp.sum(d_normed.reshape(rows // 8, 8, dim), axis=0)
+    d_xh = d_normed * gain[...]
+    mean_a = jnp.sum(d_xh, axis=1, keepdims=True) * (1.0 / dim)
+    mean_b = jnp.sum(d_xh * xh, axis=1, keepdims=True) * (1.0 / dim)
+    d_hidden[...] = (rstd * (d_xh - mean_a - xh * mean_b)).astype(jnp.bfloat16)
+
+    @pl.when(step == pl.num_programs(0) - 1)
+    def _():
+        for k in range(2):
+            total = jnp.sum(acc[k], axis=0, keepdims=True)
+            for q in range(4):
+                sums[4 * k + q:4 * k + q + 1, :] = total[:, q * (dim // 4):(q + 1) * (dim // 4)]
+
+
+def norm_back(own, from_x, from_y, hidden, ln_gain):
+    rows, dim = hidden.shape
+    blk = 64
+    half_spec = pl.BlockSpec((blk, dim // 2), lambda i: (i, 0))
+    full_spec = pl.BlockSpec((blk, dim), lambda i: (i, 0))
+    return pl.pallas_call(
+        norm_back_kernel,
+        name="norm_back",
+        grid=(rows // blk,),
+        out_shape=(jax.ShapeDtypeStruct((rows, dim), jnp.bfloat16), jax.ShapeDtypeStruct((8, dim // 4), jnp.float32)),
+        in_specs=[half_spec] * 6 + [full_spec, pl.BlockSpec((1, dim), lambda i: (0, 0))],
+        out_specs=(full_spec, pl.BlockSpec((8, dim // 4), lambda i: (0, 0))),
+        scratch_shapes=[pltpu.VMEM((2, 8, dim), jnp.float32)],
+        compiler_params=pltpu.CompilerParams(vmem_limit_bytes=40 * 1024 * 1024),
+        cost_estimate=pl.CostEstimate(flops=20 * rows * dim, bytes_accessed=rows * dim * 16, transcendentals=rows),
+    )(*own, *from_x, *from_y, hidden, ln_gain[None, :])
+
+
+def sum_kernel(mine, total, others, send_sem, recv_sem):
+    me = lax.axis_index("tp")
+    barrier = pltpu.get_barrier_semaphore()
+    for bit in range(1, 8):
+        pl.semaphore_signal(barrier, inc=1, device_id={"tp": me ^ bit}, device_id_type=MESH)
+    pl.semaphore_wait(barrier, 7)
+    copies = [pltpu.make_async_remote_copy(src_ref=mine, dst_ref=others.at[bit - 1], send_sem=send_sem.at[bit], recv_sem=recv_sem.at[bit], device_id={"tp": me ^ bit}, device_id_type=MESH) for bit in range(1, 8)]
+    for c in copies:
+        c.start()
+    for c in copies:
+        c.wait()
+    t = [mine[...]] + [others[bit - 1] for bit in range(1, 8)]
+    total[...] = ((t[0] + t[1]) + (t[2] + t[3])) + ((t[4] + t[5]) + (t[6] + t[7]))
+
+
+def small_sum(x):
+    vmem_spec = pl.BlockSpec(memory_space=pltpu.VMEM)
+    return pl.pallas_call(
+        sum_kernel,
+        name="small_sum",
+        out_shape=jax.ShapeDtypeStruct(x.shape, x.dtype),
+        in_specs=[vmem_spec],
+        out_specs=vmem_spec,
+        scratch_shapes=[pltpu.VMEM((7, *x.shape), x.dtype), pltpu.SemaphoreType.DMA((8,)), pltpu.SemaphoreType.DMA((8,))],
+        compiler_params=pltpu.CompilerParams(collective_id=1, has_side_effects=True),
+    )(x)
 
 
 def layer_norm(h_float, ln_gain, ln_bias):
@@ -326,7 +404,7 @@
         rows_loc, dim = hidden.shape
         vocab_loc = out_embed.shape[0]
         shard_idx = lax.axis_index("tp")
-        normed, ln_back = jax.vjp(layer_norm, hidden.astype(jnp.float32), ln_gain, ln_bias)
+        normed = layer_norm(hidden.astype(jnp.float32), ln_gain, ln_bias)
         meta_own = jnp.concatenate([targets.reshape(4, PIECE), loss_mask.reshape(4, PIECE)])
         x_all, grad, stats, meta = gather_logits(normed.astype(jnp.bfloat16), out_embed, meta_own, (vocab_valid != 0).astype(jnp.float32)[:, None])
         sum_exp = stats[:, :4].reshape(8, rows_loc)
@@ -337,7 +415,7 @@
         def group_sum(part):
             return ((part[0] + part[1]) + (part[2] + part[3])) + ((part[4] + part[5]) + (part[6] + part[7]))
 
-        tok_count = group_sum(jnp.sum(mask_all, axis=1))
+        tok_count = jnp.sum(mask_all)
         lse = jnp.log(sum_exp)
         loss_all = (lse - SOFT_CAP * tgt_tanh + Z_COEF * lse * lse) * mask_all
         mean_loss = group_sum(jnp.sum(loss_all, axis=1)) / tok_count
@@ -362,28 +440,26 @@
         pair_far = [part(step, 6, c) + swap(1, far[c]) for c in range(2)]
         step, *pair_far = after(step, *pair_far)
         to_x, to_y = swap(2, pair_far[0]), swap(4, pair_far[1])
-        near = [*dx_part(step, out_embed, 3), *dx_part(step, out_embed, 5)]
+        near = dx_part(step, out_embed, (3, 5))
         step, *near = after(step, *near)
-        other = dx_part(step, out_embed, 1)
+        other = dx_part(step, out_embed, (1,))
         got = [swap(1, x) for x in near]
         step, *other = after(step, *other)
-        first_x = dx_part(step, out_embed, 2, got[:2])
-        step, *first_x = after(step, *first_x)
-        first_y = dx_part(step, out_embed, 4, got[2:])
-        step, *first_y = after(step, *first_y)
+        first = dx_part(step, out_embed, (2, 4), got)
+        step, *first = after(step, *first)
+        first_x, first_y = first[:2], first[2:]
         from_x, from_y = [swap(2, first_x[0]), None], [None, swap(4, first_y[1])]
         got = [swap(1, x) for x in other]
-        own = dx_part(step, out_embed, 0, got)
+        own = dx_part(step, out_embed, (0,), got)
         step, *own = after(step, *own)
         second = [first_x[1] + to_y, first_y[0] + to_x]
         step, *second = after(step, *second)
         from_x[1], from_y[0] = swap(2, second[0]), swap(4, second[1])
         d_embed = lax.dot_general(step, x_all, (((1,), (0,)), ((), ())), preferred_element_type=jnp.float32)
-        d_normed = jnp.concatenate([own[c] + from_x[c] + from_y[c] for c in range(2)], axis=1)
-        d_hidden, gain_part, bias_part = ln_back(d_normed)
-        d_both = lax.psum(jnp.stack([gain_part, bias_part]), "tp")
+        d_hidden, sums = norm_back(own, from_x, from_y, hidden, ln_gain)
+        d_both = small_sum(sums).reshape(2, dim)
         tok_loss = loss_all[0]
-        return tok_loss, mean_loss.reshape(1), d_hidden.astype(jnp.bfloat16), d_embed, d_both[0], d_both[1]
+        return tok_loss, mean_loss.reshape(1), d_hidden, d_embed, d_both[0], d_both[1]
 
     row_spec = P(("dp", "tp"))
     mat_spec = P(("dp", "tp"), None)

time: 721 us -> 690 us (0.957)
  other arithmetic: 85.5 us -> 61.6 us
  blocking collectives: 22.4 us -> 0 us
  Pallas kernels: 342 us -> 354 us
    psum x1 -> x0, blocking collectives: 22.4 us -> none  [group_step(): d_both = lax.psum(jnp.stack([gain_part, bias_part]), 'tp')]
    pallas_call x6, Pallas kernels: 153 us -> 165 us  [the longest x4 143 us: dx_part(): pl.pallas_call(functools.partial(part_kernel, len(devs), len(adds)), name...]
    add x2 -> x0, other arithmetic: 12.4 us -> none  [group_step(): own[c] + from_x[c] + from_y[c]]
    reduce_sum x2 -> x0, other arithmetic: 9.93 us -> none  [the longest x1 5.94 us: layer_norm(): centered = h_float - mean_val]
where the time goes in v3:
time: 690 us; the launch traced here: 687 us
  Pallas kernels  354 us (51%)
  matrix products  208 us (30%)
  other arithmetic  61.6 us (9%)
  waiting for transfers between devices  37.1 us (5%)
  local copies, waits for them, and re-layouts  9.13 us (1%)
  starting transfers between devices  8.35 us (1%)
  between operations  7.93 us (1%)
    pallas_call x1, Pallas kernels, gather_logits(): pl.pallas_call(logits_kernel, name='gather_logits', out_shape=(jax.ShapeD...  189 us
    dot_general x1, matrix products, group_step(): lax.dot_general(step, x_all, (((1,), (0,)), ((), ())), preferred_element_...  151 us
    pallas_call x4, Pallas kernels, dx_part(): pl.pallas_call(functools.partial(part_kernel, len(devs), len(adds)), name...  143 us
    dot_general x4, matrix products, part(): lax.dot_general(rows, out_embed[:, c * mid:(c + 1) * mid], (((0,), (0,)),...  57.1 us
    ppermute x14, waiting for transfers between devices, swap(): return lax.ppermute(x, 'tp', [(i, i ^ bit) for i in range(8)])  37.1 us
    convert_element_type x1, other arithmetic, group_step(): (prob_coef * grad - jnp.where(is_target, tgt_coef, 0.0)).astype(jnp.bfloa...  33.6 us
    pallas_call x1, Pallas kernels, norm_back(): pl.pallas_call(norm_back_kernel, name='norm_back', grid=(rows // blk,), o...  14.9 us
  transfers between devices with their start and end apart: 14, of which 3 were waited for; matrix products, arithmetic and copies ran while one was open for 26% of the time, Pallas kernels for 14%

profile of v3, /device:TPU:0, one launch (start us, length us, event | category | flops | bytes accessed | tf_op | source)
XLA Modules:
  0.0 686.9 jit_solution(3592401503590175091)
XLA Ops:
  0.7 2.8 convert_reduce_fusion
  3.5 3.4 fusion.10
  7.0 2.0 copy.13.valid
  9.0 0.6 pad_add_fusion.meta_own
  9.6 5.3 fusion.13.x_own
  14.9 189.0 %gather_logits.1 = (bf16[4096,4096]{1,0:T(8,128)(2,1)}, f32[4096,4096]{1,0:T(8,128)}, f32[8,8,128]{2,1,0:T(8,128)}, s32[8,8,128]{2,1,0:T(8,128)}) custom-call(bf16[512,4096]{1,0:T(8,128)(2,1)} %fusion.13.x_own, bf16[4096,4096]{1,0:T(8,128)(2,1)} %refs_1_.3, s32[8,128]{1,0:T(8,128)} %pad_add_fusion.meta_own, f32[4096,1]{1,0:T(8,128)} %copy.13.valid), custom_call_target="tpu_custom_call" | custom-call | flops 137438953472 | bytes 100663296 | tf_op jit(solution)/shard_map/gather_logits/pallas_call | solution.py:253
  203.9 0.8 slice_subtract_fusion
  204.7 1.6 fusion.33
  206.3 1.4 convert_divide_fusion
  207.7 33.6 %subtract_convert_fusion.refs_0_.refs_1_ = bf16[4096,4096]{1,0:T(8,128)(2,1)} fusion(f32[4096,4096]{1,0:T(8,128)} %get-tuple-element.51, f32[4096]{0:T(1024)S(1)} %get-tuple-element.105, s32[4096]{0:T(1024)S(1)} %bitcast.36, f32[4096]{0:T(1024)S(1)} %get-tuple-element.104), kind=kLoop, calls=%fused_computation | loop fusion | flops 83886080 | bytes 100712448 | tf_op jit(solution)/shard_map/convert_element_type | solution.py:426
  241.3 12.9 %fusion.2 = f32[512,2048]{1,0:T(8,128)S(1)} fusion(bf16[4096,4096]{1,0:T(8,128)(2,1)} %refs_1_.3, bf16[4096,4096]{1,0:T(8,128)(2,1)} %subtract_convert_fusion.refs_0_.refs_1_), kind=kOutput, calls=%fused_computation.4 | convolution fusion | flops 8589934592 | bytes 25165824 | tf_op jit(solution)/shard_map/dot_general | solution.py:433
  254.3 13.5 %fusion.6 = f32[512,2048]{1,0:T(8,128)S(1)} fusion(bf16[4096,4096]{1,0:T(8,128)(2,1)} %refs_1_.3, bf16[4096,4096]{1,0:T(8,128)(2,1)} %subtract_convert_fusion.refs_0_.refs_1_), kind=kOutput, calls=%fused_computation.8 | convolution fusion | flops 8589934592 | bytes 25165824 | tf_op jit(solution)/shard_map/dot_general | solution.py:433
  267.7 0.2 collective-permute-start
  267.9 0.3 collective-permute-start.1
  268.2 6.8 collective-permute-done
  275.0 15.7 %fusion.18 = f32[512,2048]{1,0:T(8,128)} fusion(f32[512,2048]{1,0:T(8,128)} %collective-permute-done, bf16[4096,4096]{1,0:T(8,128)(2,1)} %refs_1_.3, bf16[4096,4096]{1,0:T(8,128)(2,1)} %subtract_convert_fusion.refs_0_.refs_1_), kind=kOutput, calls=%fused_computation.22 | convolution fusion | flops 8590983168 | bytes 29360128 | tf_op jit(solution)/shard_map/dot_general | solution.py:433
  290.7 15.1 %fusion.23 = f32[512,2048]{1,0:T(8,128)} fusion(f32[512,2048]{1,0:T(8,128)S(1)} %collective-permute-done.1, bf16[4096,4096]{1,0:T(8,128)(2,1)} %refs_1_.3, bf16[4096,4096]{1,0:T(8,128)(2,1)} %subtract_convert_fusion.refs_0_.refs_1_), kind=kOutput, calls=%fused_computation.23 | convolution fusion | flops 8590983168 | bytes 29360128 | tf_op jit(solution)/shard_map/dot_general | solution.py:433
  305.8 44.1 %dx_part.4 = (f32[512,2048]{1,0:T(8,128)}, f32[512,2048]{1,0:T(8,128)}, f32[512,2048]{1,0:T(8,128)}, f32[512,2048]{1,0:T(8,128)}) custom-call(bf16[4096,4096]{1,0:T(8,128)(2,1)} %subtract_convert_fusion.refs_0_.refs_1_, bf16[4096,4096]{1,0:T(8,128)(2,1)} %subtract_convert_fusion.refs_0_.refs_1_, bf16[4096,4096]{1,0:T(8,128)(2,1)} %refs_1_.3), custom_call_target="tpu_custom_call" | custom-call | flops 34359738368 | bytes 58720256 | tf_op jit(solution)/shard_map/dx_part/pallas_call | solution.py:304
  349.9 0.2 collective-permute-start.2
  350.1 0.3 collective-permute-start.3
  350.4 0.2 collective-permute-start.4
  350.6 0.3 collective-permute-start.5
  350.9 24.8 %dx_part.5 = (f32[512,2048]{1,0:T(8,128)}, f32[512,2048]{1,0:T(8,128)}) custom-call(bf16[4096,4096]{1,0:T(8,128)(2,1)} %subtract_convert_fusion.refs_0_.refs_1_, bf16[4096,4096]{1,0:T(8,128)(2,1)} %refs_1_.3), custom_call_target="tpu_custom_call" | custom-call | flops 17179869184 | bytes 46137344 | tf_op jit(solution)/shard_map/dx_part/pallas_call | solution.py:304
  375.7 0.2 collective-permute-start.6
  375.9 0.3 collective-permute-start.7
  376.3 0.7 fusion.34
  382.7 0.6 fusion.32
  383.3 0.4 collective-permute-start.9
  383.7 0.0 collective-permute-done.4.refs_5_
  383.7 0.4 collective-permute-start.10
  384.1 47.0 %dx_part.6 = (f32[512,2048]{1,0:T(8,128)}, f32[512,2048]{1,0:T(8,128)}, f32[512,2048]{1,0:T(8,128)}, f32[512,2048]{1,0:T(8,128)}) custom-call(bf16[4096,4096]{1,0:T(8,128)(2,1)} %subtract_convert_fusion.refs_0_.refs_1_, bf16[4096,4096]{1,0:T(8,128)(2,1)} %subtract_convert_fusion.refs_0_.refs_1_, bf16[4096,4096]{1,0:T(8,128)(2,1)} %refs_1_.3, ...), custom_call_target="tpu_custom_call" | custom-call | flops 34359738368 | bytes 75497472 | tf_op jit(solution)/shard_map/dx_part/pallas_call | solution.py:304
  431.1 1.6 collective-permute-start.8
  432.8 1.6 collective-permute-start.13
  434.4 26.6 %dx_part.7 = (f32[512,2048]{1,0:T(8,128)}, f32[512,2048]{1,0:T(8,128)}) custom-call(bf16[4096,4096]{1,0:T(8,128)(2,1)} %subtract_convert_fusion.refs_0_.refs_1_, bf16[4096,4096]{1,0:T(8,128)(2,1)} %refs_1_.3, f32[512,2048]{1,0:T(8,128)} %collective-permute-done.6.refs_2_, f32[512,2048]{1,0:T(8,128)} %collective-permute-done.7.refs_3_), custom_call_target="tpu_custom_call" | custom-call | flops 17179869184 | bytes 54525952 | tf_op jit(solution)/shard_map/dx_part/pallas_call | solution.py:304
  461.0 16.5 %collective-permute-done.10 = f32[512,2048]{1,0:T(8,128)} collective-permute-done((f32[512,2048]{1,0:T(8,128)}, f32[512,2048]{1,0:T(8,128)}, u32[]{:S(2)}, u32[]{:S(2)}) %collective-permute-start.10) | collective-permute-done | bytes 4194336 | tf_op jit(solution)/shard_map/ppermute | solution.py:401
  477.5 6.5 add.92
  484.0 4.9 add.91
  488.9 0.4 collective-permute-start.11
  489.3 1.9 collective-permute-start.12
  491.2 151.2 %fusion.35 = f32[4096,4096]{1,0:T(8,128)} fusion(bf16[4096,4096]{1,0:T(8,128)(2,1)} %subtract_convert_fusion.refs_0_.refs_1_, bf16[4096,4096]{1,0:T(8,128)(2,1)} %get-tuple-element.90), kind=kOutput, calls=%fused_computation.53 | convolution fusion | flops 137438953472 | bytes 134217728 | tf_op jit(solution)/shard_map/dot_general | solution.py:458
  642.4 13.8 %collective-permute-done.11.x_b = f32[512,2048]{1,0:T(8,128)} collective-permute-done((f32[512,2048]{1,0:T(8,128)}, f32[512,2048]{1,0:T(8,128)}, u32[]{:S(2)}, u32[]{:S(2)}) %collective-permute-start.11) | collective-permute-done | bytes 4194336 | tf_op jit(solution)/shard_map/ppermute | solution.py:401
  656.2 2.2 copy-done
  658.4 2.2 copy-done.1
  660.6 14.9 %norm_back.1 = (bf16[512,4096]{1,0:T(8,128)(2,1)}, f32[8,1024]{1,0:T(8,128)S(1)}) custom-call(f32[512,2048]{1,0:T(8,128)S(1)} %copy-done, f32[512,2048]{1,0:T(8,128)S(1)} %copy-done.1, f32[512,2048]{1,0:T(8,128)} %collective-permute-done.8.x_a, f32[512,2048]{1,0:T(8,128)} %collective-permute-done.11.x_b, f32[512,2048]{1,0:T(8,128)} %collective-permute-done.12.y_a, ...), custom_call_target="tpu_custom_call" | custom-call | flops 41943040 | bytes 33554432 | tf_op jit(solution)/shard_map/norm_back/pallas_call | solution.py:351
  675.4 0.6 copy-done.3
  676.1 8.0 %small_sum.1 = f32[8,1024]{1,0:T(8,128)} custom-call(f32[8,1024]{1,0:T(8,128)} %copy-done.3), custom_call_target="tpu_custom_call" | custom-call | tf_op jit(solution)/shard_map/small_sum/pallas_call | solution.py:381
  684.1 0.8 slice_bitcast_fusion
  685.0 0.6 copy_bitcast_fusion
  (31 shorter events, 0.1 us)
Async XLA Ops:
  0.6 6.3 copy-start.6
  0.6 8.3 %copy-start.7 = (s32[512]{0:T(512)S(1)}, s32[512]{0:T(512)}, u32[]{:S(2)}) copy-start(s32[512]{0:T(512)} %param.13) | copy-start | bytes 6148
  0.7 8.3 %copy-start.8 = (s32[512]{0:T(512)S(1)}, s32[512]{0:T(512)}, u32[]{:S(2)}) copy-start(s32[512]{0:T(512)} %param.12) | copy-start | bytes 6148
  0.7 8.9 %copy-start.2 = (f32[4096]{0:T(1024)S(1)}, f32[4096]{0:T(1024)}, u32[]{:S(2)}) copy-start(f32[4096]{0:T(1024)} %param.8) | copy-start | bytes 49156
  0.7 8.9 %copy-start.5 = (f32[4096]{0:T(1024)S(1)}, f32[4096]{0:T(1024)}, u32[]{:S(2)}) copy-start(f32[4096]{0:T(1024)} %param.9) | copy-start | bytes 49156
  267.7 7.3 %collective-permute-start = (f32[512,2048]{1,0:T(8,128)S(1)}, f32[512,2048]{1,0:T(8,128)}, u32[]{:S(2)}, u32[]{:S(2)}) collective-permute-start(f32[512,2048]{1,0:T(8,128)S(1)} %fusion.6), channel_id=1, source_target_pairs={{0,1},{1,0},{2,3},{3,2},{4,5},{5,4},{6,7},{7,6}} | collective-permute-start | bytes 12582920 | tf_op jit(solution)/shard_map/ppermute | solution.py:401
  267.9 22.8 %collective-permute-start.1 = (f32[512,2048]{1,0:T(8,128)S(1)}, f32[512,2048]{1,0:T(8,128)S(1)}, u32[]{:S(2)}, u32[]{:S(2)}) collective-permute-start(f32[512,2048]{1,0:T(8,128)S(1)} %fusion.2), channel_id=1, source_target_pairs={{0,1},{1,0},{2,3},{3,2},{4,5},{5,4},{6,7},{7,6}} | collective-permute-start | bytes 12582920 | tf_op jit(solution)/shard_map/ppermute | solution.py:401
  349.9 26.0 %collective-permute-start.2 = (f32[512,2048]{1,0:T(8,128)}, f32[512,2048]{1,0:T(8,128)}, u32[]{:S(2)}, u32[]{:S(2)}) collective-permute-start(f32[512,2048]{1,0:T(8,128)} %get-tuple-element.64), channel_id=1, source_target_pairs={{0,1},{1,0},{2,3},{3,2},{4,5},{5,4},{6,7},{7,6}} | collective-permute-start | bytes 12582920 | tf_op jit(solution)/shard_map/ppermute | solution.py:401
  350.1 33.3 %collective-permute-start.3 = (f32[512,2048]{1,0:T(8,128)}, f32[512,2048]{1,0:T(8,128)}, u32[]{:S(2)}, u32[]{:S(2)}) collective-permute-start(f32[512,2048]{1,0:T(8,128)} %get-tuple-element.65), channel_id=1, source_target_pairs={{0,1},{1,0},{2,3},{3,2},{4,5},{5,4},{6,7},{7,6}} | collective-permute-start | bytes 12582920 | tf_op jit(solution)/shard_map/ppermute | solution.py:401
  350.4 33.4 %collective-permute-start.4 = (f32[512,2048]{1,0:T(8,128)}, f32[512,2048]{1,0:T(8,128)}, u32[]{:S(2)}, u32[]{:S(2)}) collective-permute-start(f32[512,2048]{1,0:T(8,128)} %get-tuple-element.66), channel_id=1, source_target_pairs={{0,1},{1,0},{2,3},{3,2},{4,5},{5,4},{6,7},{7,6}} | collective-permute-start | bytes 12582920 | tf_op jit(solution)/shard_map/ppermute | solution.py:401
  350.6 33.5 %collective-permute-start.5 = (f32[512,2048]{1,0:T(8,128)}, f32[512,2048]{1,0:T(8,128)}, u32[]{:S(2)}, u32[]{:S(2)}) collective-permute-start(f32[512,2048]{1,0:T(8,128)} %get-tuple-element.67), channel_id=1, source_target_pairs={{0,1},{1,0},{2,3},{3,2},{4,5},{5,4},{6,7},{7,6}} | collective-permute-start | bytes 12582920 | tf_op jit(solution)/shard_map/ppermute | solution.py:401
  375.7 57.0 %collective-permute-start.6 = (f32[512,2048]{1,0:T(8,128)}, f32[512,2048]{1,0:T(8,128)}, u32[]{:S(2)}, u32[]{:S(2)}) collective-permute-start(f32[512,2048]{1,0:T(8,128)} %get-tuple-element.73), channel_id=1, source_target_pairs={{0,1},{1,0},{2,3},{3,2},{4,5},{5,4},{6,7},{7,6}} | collective-permute-start | bytes 12582920 | tf_op jit(solution)/shard_map/ppermute | solution.py:401
  375.9 58.5 %collective-permute-start.7 = (f32[512,2048]{1,0:T(8,128)}, f32[512,2048]{1,0:T(8,128)}, u32[]{:S(2)}, u32[]{:S(2)}) collective-permute-start(f32[512,2048]{1,0:T(8,128)} %get-tuple-element.74), channel_id=1, source_target_pairs={{0,1},{1,0},{2,3},{3,2},{4,5},{5,4},{6,7},{7,6}} | collective-permute-start | bytes 12582920 | tf_op jit(solution)/shard_map/ppermute | solution.py:401
  383.3 100.7 %collective-permute-start.9 = (f32[512,2048]{1,0:T(8,128)}, f32[512,2048]{1,0:T(8,128)}, u32[]{:S(2)}, u32[]{:S(2)}) collective-permute-start(f32[512,2048]{1,0:T(8,128)} %fusion.23), channel_id=1, source_target_pairs={{0,4},{1,5},{2,6},{3,7},{4,0},{5,1},{6,2},{7,3}} | collective-permute-start | bytes 12582920 | tf_op jit(solution)/shard_map/ppermute | solution.py:401
  383.7 93.8 %collective-permute-start.10 = (f32[512,2048]{1,0:T(8,128)}, f32[512,2048]{1,0:T(8,128)}, u32[]{:S(2)}, u32[]{:S(2)}) collective-permute-start(f32[512,2048]{1,0:T(8,128)} %fusion.18), channel_id=1, source_target_pairs={{0,2},{1,3},{2,0},{3,1},{4,6},{5,7},{6,4},{7,5}} | collective-permute-start | bytes 12582920 | tf_op jit(solution)/shard_map/ppermute | solution.py:401
  431.1 211.2 %collective-permute-start.8 = (f32[512,2048]{1,0:T(8,128)}, f32[512,2048]{1,0:T(8,128)}, u32[]{:S(2)}, u32[]{:S(2)}) collective-permute-start(f32[512,2048]{1,0:T(8,128)} %get-tuple-element.79), channel_id=1, source_target_pairs={{0,2},{1,3},{2,0},{3,1},{4,6},{5,7},{6,4},{7,5}} | collective-permute-start | bytes 12582920 | tf_op jit(solution)/shard_map/ppermute | solution.py:401
  432.8 209.6 %collective-permute-start.13 = (f32[512,2048]{1,0:T(8,128)}, f32[512,2048]{1,0:T(8,128)}, u32[]{:S(2)}, u32[]{:S(2)}) collective-permute-start(f32[512,2048]{1,0:T(8,128)} %get-tuple-element.87), channel_id=1, source_target_pairs={{0,4},{1,5},{2,6},{3,7},{4,0},{5,1},{6,2},{7,3}} | collective-permute-start | bytes 12582920 | tf_op jit(solution)/shard_map/ppermute | solution.py:401
  461.0 23.0 %copy-start.4 = (f32[512,2048]{1,0:T(8,128)S(1)}, f32[512,2048]{1,0:T(8,128)}, u32[]{:S(2)}) copy-start(f32[512,2048]{1,0:T(8,128)} %get-tuple-element.81) | copy-start | bytes 12582916
  488.9 167.2 %collective-permute-start.11 = (f32[512,2048]{1,0:T(8,128)}, f32[512,2048]{1,0:T(8,128)}, u32[]{:S(2)}, u32[]{:S(2)}) collective-permute-start(f32[512,2048]{1,0:T(8,128)} %add.91), channel_id=1, source_target_pairs={{0,2},{1,3},{2,0},{3,1},{4,6},{5,7},{6,4},{7,5}} | collective-permute-start | bytes 12582920 | tf_op jit(solution)/shard_map/ppermute | solution.py:401
  489.3 166.9 %collective-permute-start.12 = (f32[512,2048]{1,0:T(8,128)}, f32[512,2048]{1,0:T(8,128)}, u32[]{:S(2)}, u32[]{:S(2)}) collective-permute-start(f32[512,2048]{1,0:T(8,128)} %add.92), channel_id=1, source_target_pairs={{0,4},{1,5},{2,6},{3,7},{4,0},{5,1},{6,2},{7,3}} | collective-permute-start | bytes 12582920 | tf_op jit(solution)/shard_map/ppermute | solution.py:401
  656.2 2.2 copy-start
  658.4 2.2 copy-start.1
  675.4 0.6 copy-start.3

commit v4 on v3

--- a/solution.py
+++ b/solution.py
@@ -389,11 +389,29 @@
     )(x)
 
 
-def layer_norm(h_float, ln_gain, ln_bias):
-    mean_val = jnp.mean(h_float, axis=-1, keepdims=True)
-    centered = h_float - mean_val
-    var_val = jnp.mean(centered * centered, axis=-1, keepdims=True)
-    return centered * lax.rsqrt(var_val + LN_EPS) * ln_gain + ln_bias
+def norm_kernel(hidden, gain, bias, x):
+    h = hidden[...].astype(jnp.float32)
+    dim = h.shape[1]
+    centered = h - jnp.sum(h, axis=1, keepdims=True) * (1.0 / dim)
+    rstd = lax.rsqrt(jnp.sum(centered * centered, axis=1, keepdims=True) * (1.0 / dim) + LN_EPS)
+    x[...] = (centered * rstd * gain[...] + bias[...]).astype(jnp.bfloat16)
+
+
+def norm_forward(hidden, ln_gain, ln_bias):
+    rows, dim = hidden.shape
+    blk = 64
+    full_spec = pl.BlockSpec((blk, dim), lambda i: (i, 0))
+    row_spec = pl.BlockSpec((1, dim), lambda i: (0, 0))
+    return pl.pallas_call(
+        norm_kernel,
+        name="norm_forward",
+        grid=(rows // blk,),
+        out_shape=jax.ShapeDtypeStruct((rows, dim), jnp.bfloat16),
+        in_specs=[full_spec, row_spec, row_spec],
+        out_specs=full_spec,
+        compiler_params=pltpu.CompilerParams(vmem_limit_bytes=32 * 1024 * 1024),
+        cost_estimate=pl.CostEstimate(flops=8 * rows * dim, bytes_accessed=rows * dim * 4, transcendentals=rows),
+    )(hidden, ln_gain[None, :], ln_bias[None, :])
 
 
 def solution(mesh):
@@ -404,9 +422,9 @@
         rows_loc, dim = hidden.shape
         vocab_loc = out_embed.shape[0]
         shard_idx = lax.axis_index("tp")
-        normed = layer_norm(hidden.astype(jnp.float32), ln_gain, ln_bias)
+        normed = norm_forward(hidden, ln_gain, ln_bias)
         meta_own = jnp.concatenate([targets.reshape(4, PIECE), loss_mask.reshape(4, PIECE)])
-        x_all, grad, stats, meta = gather_logits(normed.astype(jnp.bfloat16), out_embed, meta_own, (vocab_valid != 0).astype(jnp.float32)[:, None])
+        x_all, grad, stats, meta = gather_logits(normed, out_embed, meta_own, (vocab_valid != 0).astype(jnp.float32)[:, None])
         sum_exp = stats[:, :4].reshape(8, rows_loc)
         tgt_tanh = stats[:, 4:].reshape(8, rows_loc)
         tgt_row = meta[:, :4].reshape(8 * rows_loc) - shard_idx * vocab_loc

time: 690 us -> 696 us (level)
  other arithmetic: 61.6 us -> 51.6 us
where the time goes in v4:
time: 696 us; the launch traced here: 686 us
  Pallas kernels  358 us (51%)
  matrix products  208 us (30%)
  other arithmetic  51.6 us (7%)
  waiting for transfers between devices  37.3 us (5%)
  local copies, waits for them, and re-layouts  14.7 us (2%)
  starting transfers between devices  8.36 us (1%)
  between operations  7.87 us (1%)
    pallas_call x1, Pallas kernels, gather_logits(): pl.pallas_call(logits_kernel, name='gather_logits', out_shape=(jax.ShapeD...  189 us
    dot_general x1, matrix products, group_step(): lax.dot_general(step, x_all, (((1,), (0,)), ((), ())), preferred_element_...  151 us
    pallas_call x4, Pallas kernels, dx_part(): pl.pallas_call(functools.partial(part_kernel, len(devs), len(adds)), name...  142 us
    dot_general x4, matrix products, part(): lax.dot_general(rows, out_embed[:, c * mid:(c + 1) * mid], (((0,), (0,)),...  57.1 us
    ppermute x14, waiting for transfers between devices, swap(): return lax.ppermute(x, 'tp', [(i, i ^ bit) for i in range(8)])  37.3 us
    convert_element_type x1, other arithmetic, group_step(): (prob_coef * grad - jnp.where(is_target, tgt_coef, 0.0)).astype(jnp.bfloa...  33.6 us
    pallas_call x1, Pallas kernels, norm_back(): pl.pallas_call(norm_back_kernel, name='norm_back', grid=(rows // blk,), o...  14.9 us
  transfers between devices with their start and end apart: 14, of which 3 were waited for; matrix products, arithmetic and copies ran while one was open for 26% of the time, Pallas kernels for 14%

profile of v4, /device:TPU:0, one launch (start us, length us, event | category | flops | bytes accessed | tf_op | source)
XLA Modules:
  0.0 686.4 jit_solution(2987546552265322218)
XLA Ops:
  0.6 0.7 compare_convert_fusion
  1.4 2.0 copy.13.valid
  3.3 1.3 pad_add_fusion.meta_own
  4.6 2.2 copy-done
  6.8 0.7 copy-done.4
  7.5 0.7 copy-done.7
  8.3 4.3 norm_forward.1.x_own
  12.5 2.0 copy-done.3
  14.5 188.9 %gather_logits.1 = (bf16[4096,4096]{1,0:T(8,128)(2,1)}, f32[4096,4096]{1,0:T(8,128)}, f32[8,8,128]{2,1,0:T(8,128)}, s32[8,8,128]{2,1,0:T(8,128)}) custom-call(bf16[512,4096]{1,0:T(8,128)(2,1)} %copy-done.3, bf16[4096,4096]{1,0:T(8,128)(2,1)} %refs_1_.3, s32[8,128]{1,0:T(8,128)} %pad_add_fusion.meta_own, f32[4096,1]{1,0:T(8,128)} %copy.13.valid), custom_call_target="tpu_custom_call" | custom-call | flops 137438953472 | bytes 100663296 | tf_op jit(solution)/shard_map/gather_logits/pallas_call | solution.py:253
  203.5 0.8 slice_subtract_fusion
  204.3 1.6 fusion.27
  205.9 1.4 convert_divide_fusion
  207.3 33.6 %subtract_convert_fusion.refs_0_.refs_1_ = bf16[4096,4096]{1,0:T(8,128)(2,1)} fusion(f32[4096,4096]{1,0:T(8,128)} %get-tuple-element.51, f32[4096]{0:T(1024)S(1)} %get-tuple-element.105, s32[4096]{0:T(1024)S(1)} %bitcast.39, f32[4096]{0:T(1024)S(1)} %get-tuple-element.104), kind=kLoop, calls=%fused_computation | loop fusion | flops 83886080 | bytes 100712448 | tf_op jit(solution)/shard_map/convert_element_type | solution.py:444
  241.0 12.9 %fusion.2 = f32[512,2048]{1,0:T(8,128)S(1)} fusion(bf16[4096,4096]{1,0:T(8,128)(2,1)} %refs_1_.3, bf16[4096,4096]{1,0:T(8,128)(2,1)} %subtract_convert_fusion.refs_0_.refs_1_), kind=kOutput, calls=%fused_computation.4 | convolution fusion | flops 8589934592 | bytes 25165824 | tf_op jit(solution)/shard_map/dot_general | solution.py:451
  253.9 13.4 %fusion.6 = f32[512,2048]{1,0:T(8,128)S(1)} fusion(bf16[4096,4096]{1,0:T(8,128)(2,1)} %refs_1_.3, bf16[4096,4096]{1,0:T(8,128)(2,1)} %subtract_convert_fusion.refs_0_.refs_1_), kind=kOutput, calls=%fused_computation.8 | convolution fusion | flops 8589934592 | bytes 25165824 | tf_op jit(solution)/shard_map/dot_general | solution.py:451
  267.3 0.2 collective-permute-start
  267.5 0.4 collective-permute-start.1
  267.9 6.8 collective-permute-done
  274.6 15.7 %fusion.12 = f32[512,2048]{1,0:T(8,128)} fusion(f32[512,2048]{1,0:T(8,128)} %collective-permute-done, bf16[4096,4096]{1,0:T(8,128)(2,1)} %refs_1_.3, bf16[4096,4096]{1,0:T(8,128)(2,1)} %subtract_convert_fusion.refs_0_.refs_1_), kind=kOutput, calls=%fused_computation.14 | convolution fusion | flops 8590983168 | bytes 29360128 | tf_op jit(solution)/shard_map/dot_general | solution.py:451
  290.3 15.0 %fusion.17 = f32[512,2048]{1,0:T(8,128)} fusion(f32[512,2048]{1,0:T(8,128)S(1)} %collective-permute-done.1, bf16[4096,4096]{1,0:T(8,128)(2,1)} %refs_1_.3, bf16[4096,4096]{1,0:T(8,128)(2,1)} %subtract_convert_fusion.refs_0_.refs_1_), kind=kOutput, calls=%fused_computation.15 | convolution fusion | flops 8590983168 | bytes 29360128 | tf_op jit(solution)/shard_map/dot_general | solution.py:451
  305.4 44.0 %dx_part.4 = (f32[512,2048]{1,0:T(8,128)}, f32[512,2048]{1,0:T(8,128)}, f32[512,2048]{1,0:T(8,128)}, f32[512,2048]{1,0:T(8,128)}) custom-call(bf16[4096,4096]{1,0:T(8,128)(2,1)} %subtract_convert_fusion.refs_0_.refs_1_, bf16[4096,4096]{1,0:T(8,128)(2,1)} %subtract_convert_fusion.refs_0_.refs_1_, bf16[4096,4096]{1,0:T(8,128)(2,1)} %refs_1_.3), custom_call_target="tpu_custom_call" | custom-call | flops 34359738368 | bytes 58720256 | tf_op jit(solution)/shard_map/dx_part/pallas_call | solution.py:304
  349.4 0.2 collective-permute-start.2
  349.6 0.4 collective-permute-start.3
  350.1 0.4 collective-permute-start.5
  350.4 24.8 %dx_part.5 = (f32[512,2048]{1,0:T(8,128)}, f32[512,2048]{1,0:T(8,128)}) custom-call(bf16[4096,4096]{1,0:T(8,128)(2,1)} %subtract_convert_fusion.refs_0_.refs_1_, bf16[4096,4096]{1,0:T(8,128)(2,1)} %refs_1_.3), custom_call_target="tpu_custom_call" | custom-call | flops 17179869184 | bytes 46137344 | tf_op jit(solution)/shard_map/dx_part/pallas_call | solution.py:304
  375.4 0.4 collective-permute-start.7
  375.8 0.7 fusion.28
  382.3 0.6 fusion.26
  382.8 0.4 collective-permute-start.9
  383.3 0.4 collective-permute-start.10
  383.6 46.9 %dx_part.6 = (f32[512,2048]{1,0:T(8,128)}, f32[512,2048]{1,0:T(8,128)}, f32[512,2048]{1,0:T(8,128)}, f32[512,2048]{1,0:T(8,128)}) custom-call(bf16[4096,4096]{1,0:T(8,128)(2,1)} %subtract_convert_fusion.refs_0_.refs_1_, bf16[4096,4096]{1,0:T(8,128)(2,1)} %subtract_convert_fusion.refs_0_.refs_1_, bf16[4096,4096]{1,0:T(8,128)(2,1)} %refs_1_.3, ...), custom_call_target="tpu_custom_call" | custom-call | flops 34359738368 | bytes 75497472 | tf_op jit(solution)/shard_map/dx_part/pallas_call | solution.py:304
  430.5 1.7 collective-permute-start.8
  432.2 1.6 collective-permute-start.13
  433.8 26.5 %dx_part.7 = (f32[512,2048]{1,0:T(8,128)}, f32[512,2048]{1,0:T(8,128)}) custom-call(bf16[4096,4096]{1,0:T(8,128)(2,1)} %subtract_convert_fusion.refs_0_.refs_1_, bf16[4096,4096]{1,0:T(8,128)(2,1)} %refs_1_.3, f32[512,2048]{1,0:T(8,128)} %collective-permute-done.6.refs_2_, f32[512,2048]{1,0:T(8,128)} %collective-permute-done.7.refs_3_), custom_call_target="tpu_custom_call" | custom-call | flops 17179869184 | bytes 54525952 | tf_op jit(solution)/shard_map/dx_part/pallas_call | solution.py:304
  460.3 16.7 %collective-permute-done.10 = f32[512,2048]{1,0:T(8,128)} collective-permute-done((f32[512,2048]{1,0:T(8,128)}, f32[512,2048]{1,0:T(8,128)}, u32[]{:S(2)}, u32[]{:S(2)}) %collective-permute-start.10) | collective-permute-done | bytes 4194336 | tf_op jit(solution)/shard_map/ppermute | solution.py:419
  477.0 6.5 add.69
  483.5 5.0 add.68
  488.5 0.4 collective-permute-start.11
  488.9 1.9 collective-permute-start.12
  490.8 151.2 %fusion.29 = f32[4096,4096]{1,0:T(8,128)} fusion(bf16[4096,4096]{1,0:T(8,128)(2,1)} %subtract_convert_fusion.refs_0_.refs_1_, bf16[4096,4096]{1,0:T(8,128)(2,1)} %get-tuple-element.90), kind=kOutput, calls=%fused_computation.43 | convolution fusion | flops 137438953472 | bytes 134217728 | tf_op jit(solution)/shard_map/dot_general | solution.py:476
  641.9 13.8 %collective-permute-done.11.x_b = f32[512,2048]{1,0:T(8,128)} collective-permute-done((f32[512,2048]{1,0:T(8,128)}, f32[512,2048]{1,0:T(8,128)}, u32[]{:S(2)}, u32[]{:S(2)}) %collective-permute-start.11) | collective-permute-done | bytes 4194336 | tf_op jit(solution)/shard_map/ppermute | solution.py:419
  655.7 2.2 copy-done.1
  657.9 2.2 copy-done.2
  660.1 14.9 %norm_back.1 = (bf16[512,4096]{1,0:T(8,128)(2,1)}, f32[8,1024]{1,0:T(8,128)S(1)}) custom-call(f32[512,2048]{1,0:T(8,128)S(1)} %copy-done.1, f32[512,2048]{1,0:T(8,128)S(1)} %copy-done.2, f32[512,2048]{1,0:T(8,128)} %collective-permute-done.8.x_a, f32[512,2048]{1,0:T(8,128)} %collective-permute-done.11.x_b, f32[512,2048]{1,0:T(8,128)} %collective-permute-done.12.y_a, ...), custom_call_target="tpu_custom_call" | custom-call | flops 41943040 | bytes 33554432 | tf_op jit(solution)/shard_map/norm_back/pallas_call | solution.py:351
  674.9 0.6 copy-done.6
  675.5 8.0 %small_sum.1 = f32[8,1024]{1,0:T(8,128)} custom-call(f32[8,1024]{1,0:T(8,128)} %copy-done.6), custom_call_target="tpu_custom_call" | custom-call | tf_op jit(solution)/shard_map/small_sum/pallas_call | solution.py:381
  683.6 0.8 slice_bitcast_fusion
  684.4 0.6 copy_bitcast_fusion
  (27 shorter events, 0.4 us)
Async XLA Ops:
  4.6 2.2 copy-start
  6.8 0.7 copy-start.4
  7.5 0.7 copy-start.7
  12.5 2.0 copy-start.3
  267.3 7.3 %collective-permute-start = (f32[512,2048]{1,0:T(8,128)S(1)}, f32[512,2048]{1,0:T(8,128)}, u32[]{:S(2)}, u32[]{:S(2)}) collective-permute-start(f32[512,2048]{1,0:T(8,128)S(1)} %fusion.6), channel_id=1, source_target_pairs={{0,1},{1,0},{2,3},{3,2},{4,5},{5,4},{6,7},{7,6}} | collective-permute-start | bytes 12582920 | tf_op jit(solution)/shard_map/ppermute | solution.py:419
  267.5 22.8 %collective-permute-start.1 = (f32[512,2048]{1,0:T(8,128)S(1)}, f32[512,2048]{1,0:T(8,128)S(1)}, u32[]{:S(2)}, u32[]{:S(2)}) collective-permute-start(f32[512,2048]{1,0:T(8,128)S(1)} %fusion.2), channel_id=1, source_target_pairs={{0,1},{1,0},{2,3},{3,2},{4,5},{5,4},{6,7},{7,6}} | collective-permute-start | bytes 12582920 | tf_op jit(solution)/shard_map/ppermute | solution.py:419
  349.4 26.0 %collective-permute-start.2 = (f32[512,2048]{1,0:T(8,128)}, f32[512,2048]{1,0:T(8,128)}, u32[]{:S(2)}, u32[]{:S(2)}) collective-permute-start(f32[512,2048]{1,0:T(8,128)} %get-tuple-element.64), channel_id=1, source_target_pairs={{0,1},{1,0},{2,3},{3,2},{4,5},{5,4},{6,7},{7,6}} | collective-permute-start | bytes 12582920 | tf_op jit(solution)/shard_map/ppermute | solution.py:419
  349.6 33.3 %collective-permute-start.3 = (f32[512,2048]{1,0:T(8,128)}, f32[512,2048]{1,0:T(8,128)}, u32[]{:S(2)}, u32[]{:S(2)}) collective-permute-start(f32[512,2048]{1,0:T(8,128)} %get-tuple-element.65), channel_id=1, source_target_pairs={{0,1},{1,0},{2,3},{3,2},{4,5},{5,4},{6,7},{7,6}} | collective-permute-start | bytes 12582920 | tf_op jit(solution)/shard_map/ppermute | solution.py:419
  349.9 33.3 %collective-permute-start.4 = (f32[512,2048]{1,0:T(8,128)}, f32[512,2048]{1,0:T(8,128)}, u32[]{:S(2)}, u32[]{:S(2)}) collective-permute-start(f32[512,2048]{1,0:T(8,128)} %get-tuple-element.66), channel_id=1, source_target_pairs={{0,1},{1,0},{2,3},{3,2},{4,5},{5,4},{6,7},{7,6}} | collective-permute-start | bytes 12582920 | tf_op jit(solution)/shard_map/ppermute | solution.py:419
  350.1 33.5 %collective-permute-start.5 = (f32[512,2048]{1,0:T(8,128)}, f32[512,2048]{1,0:T(8,128)}, u32[]{:S(2)}, u32[]{:S(2)}) collective-permute-start(f32[512,2048]{1,0:T(8,128)} %get-tuple-element.67), channel_id=1, source_target_pairs={{0,1},{1,0},{2,3},{3,2},{4,5},{5,4},{6,7},{7,6}} | collective-permute-start | bytes 12582920 | tf_op jit(solution)/shard_map/ppermute | solution.py:419
  375.3 56.9 %collective-permute-start.6 = (f32[512,2048]{1,0:T(8,128)}, f32[512,2048]{1,0:T(8,128)}, u32[]{:S(2)}, u32[]{:S(2)}) collective-permute-start(f32[512,2048]{1,0:T(8,128)} %get-tuple-element.73), channel_id=1, source_target_pairs={{0,1},{1,0},{2,3},{3,2},{4,5},{5,4},{6,7},{7,6}} | collective-permute-start | bytes 12582920 | tf_op jit(solution)/shard_map/ppermute | solution.py:419
  375.4 58.4 %collective-permute-start.7 = (f32[512,2048]{1,0:T(8,128)}, f32[512,2048]{1,0:T(8,128)}, u32[]{:S(2)}, u32[]{:S(2)}) collective-permute-start(f32[512,2048]{1,0:T(8,128)} %get-tuple-element.74), channel_id=1, source_target_pairs={{0,1},{1,0},{2,3},{3,2},{4,5},{5,4},{6,7},{7,6}} | collective-permute-start | bytes 12582920 | tf_op jit(solution)/shard_map/ppermute | solution.py:419
  382.8 100.7 %collective-permute-start.9 = (f32[512,2048]{1,0:T(8,128)}, f32[512,2048]{1,0:T(8,128)}, u32[]{:S(2)}, u32[]{:S(2)}) collective-permute-start(f32[512,2048]{1,0:T(8,128)} %fusion.17), channel_id=1, source_target_pairs={{0,4},{1,5},{2,6},{3,7},{4,0},{5,1},{6,2},{7,3}} | collective-permute-start | bytes 12582920 | tf_op jit(solution)/shard_map/ppermute | solution.py:419
  383.3 93.8 %collective-permute-start.10 = (f32[512,2048]{1,0:T(8,128)}, f32[512,2048]{1,0:T(8,128)}, u32[]{:S(2)}, u32[]{:S(2)}) collective-permute-start(f32[512,2048]{1,0:T(8,128)} %fusion.12), channel_id=1, source_target_pairs={{0,2},{1,3},{2,0},{3,1},{4,6},{5,7},{6,4},{7,5}} | collective-permute-start | bytes 12582920 | tf_op jit(solution)/shard_map/ppermute | solution.py:419
  430.5 211.4 %collective-permute-start.8 = (f32[512,2048]{1,0:T(8,128)}, f32[512,2048]{1,0:T(8,128)}, u32[]{:S(2)}, u32[]{:S(2)}) collective-permute-start(f32[512,2048]{1,0:T(8,128)} %get-tuple-element.79), channel_id=1, source_target_pairs={{0,2},{1,3},{2,0},{3,1},{4,6},{5,7},{6,4},{7,5}} | collective-permute-start | bytes 12582920 | tf_op jit(solution)/shard_map/ppermute | solution.py:419
  432.2 209.8 %collective-permute-start.13 = (f32[512,2048]{1,0:T(8,128)}, f32[512,2048]{1,0:T(8,128)}, u32[]{:S(2)}, u32[]{:S(2)}) collective-permute-start(f32[512,2048]{1,0:T(8,128)} %get-tuple-element.87), channel_id=1, source_target_pairs={{0,4},{1,5},{2,6},{3,7},{4,0},{5,1},{6,2},{7,3}} | collective-permute-start | bytes 12582920 | tf_op jit(solution)/shard_map/ppermute | solution.py:419
  460.3 23.2 %copy-start.8 = (f32[512,2048]{1,0:T(8,128)S(1)}, f32[512,2048]{1,0:T(8,128)}, u32[]{:S(2)}) copy-start(f32[512,2048]{1,0:T(8,128)} %get-tuple-element.81) | copy-start | bytes 12582916
  488.5 167.2 %collective-permute-start.11 = (f32[512,2048]{1,0:T(8,128)}, f32[512,2048]{1,0:T(8,128)}, u32[]{:S(2)}, u32[]{:S(2)}) collective-permute-start(f32[512,2048]{1,0:T(8,128)} %add.68), channel_id=1, source_target_pairs={{0,2},{1,3},{2,0},{3,1},{4,6},{5,7},{6,4},{7,5}} | collective-permute-start | bytes 12582920 | tf_op jit(solution)/shard_map/ppermute | solution.py:419
  488.9 166.8 %collective-permute-start.12 = (f32[512,2048]{1,0:T(8,128)}, f32[512,2048]{1,0:T(8,128)}, u32[]{:S(2)}, u32[]{:S(2)}) collective-permute-start(f32[512,2048]{1,0:T(8,128)} %add.69), channel_id=1, source_target_pairs={{0,4},{1,5},{2,6},{3,7},{4,0},{5,1},{6,2},{7,3}} | collective-permute-start | bytes 12582920 | tf_op jit(solution)/shard_map/ppermute | solution.py:419
  490.8 164.9 %copy-start.5 = (f32[4096]{0:T(1024)S(1)}, f32[4096]{0:T(1024)}, u32[]{:S(2)}) copy-start(f32[4096]{0:T(1024)} %param.8) | copy-start | bytes 49156
  655.7 2.2 copy-start.1
  657.9 2.2 copy-start.2
  674.9 0.6 copy-start.6
